TPU v7x, 32 devices: a whole 2x2x4 slice. The times are simulated.
32 devices in a mesh: groups: 2 (over x), seq: 4 (over y, core), dp: 4 (over z).
Axes of the slice: x: 2, y: 2, z: 4, core: 2. Of those that a mesh axis runs over, the one named last changes fastest.
Arguments:
- resid: bfloat16 [8, 256, 2048], P(('groups', 'dp'), 'seq'), parts along dimension 0, may hold values from -6 to 6
- queries_keys: bfloat16 [2, 8, 256, 2048], P(None, ('groups', 'dp'), 'seq'), parts along dimension 1, may hold values from -20 to 20
- values: bfloat16 [8, 256, 2048], P(('groups', 'dp'), 'seq'), parts along dimension 0, may hold values from -6 to 6
- doc_ids: int32 [8, 256], P(('groups', 'dp')), parts along dimension 0, may hold values from 0 to 5, never falling along the last dimension, each value on 1 to 128 neighbouring positions
- out_weight: bfloat16 [2048, 2048], P(None, 'dp'), may hold values from -0.125 to 0.125
- norm_gain: float32 [2048], replicated, may hold values from 0.5 to 1.5
- expert_ids: int32 [8, 256, 4], P(('groups', 'dp'), 'seq'), parts along dimension 0, may hold values from 0 to 31, all different within a row; in each aligned block of 64 rows (0 to 63, 64 to 127, ..., all dimensions but the last counted through in order) at most 10 rows name the same one
- gate_vals: float32 [8, 256, 4], P(('groups', 'dp'), 'seq'), parts along dimension 0, may hold values from 0.05 to 0.6
- expert_gate: bfloat16 [128, 2048, 352], P(('seq', 'dp')), may hold values from -0.125 to 0.125
- expert_up: bfloat16 [128, 2048, 352], P(('seq', 'dp')), may hold values from -0.125 to 0.125
- expert_down: bfloat16 [128, 352, 2048], P(('seq', 'dp')), may hold values from -0.15625 to 0.15625
- shared_gate: bfloat16 [2048, 2816], P(None, 'dp'), may hold values from -0.125 to 0.125
- shared_up: bfloat16 [2048, 2816], P(None, 'dp'), may hold values from -0.125 to 0.125
- shared_down: bfloat16 [2816, 2048], P('dp'), may hold values from -0.109375 to 0.109375
- shared_score: bfloat16 [2048], replicated, may hold values from -0.125 to 0.125
Outputs:
- layer_out: bfloat16 [8, 256, 2048], P(('groups', 'dp'), 'seq'), parts along dimension 0
There are 2 independent parts, one for each index of `groups`. A program takes and returns all parts, laid end to end along the dimension named above; an argument that names none is the same for every part. Nothing has to cross between parts.
Inputs may be any that keep to these rules, and one draw needn't show every extreme that they name: `doc_ids`: document numbers never fall along a sequence; each document holds 1 to 128 positions. `expert_ids`: each token names 4 different experts; among the rows of one device no expert is named more than 10 times.
All inputs are finite; a program needn't handle non-finite values.
Results may differ from a plain program's by a relative error of at most 0.01.
Values may be sent and summed in bfloat16 or wider, within the bound.
A program may use at most 128 MiB of HBM per device.

v0:
```python
import math

import jax
import jax.numpy as jnp
from jax import lax
from jax.sharding import PartitionSpec as P

HD = 128
EXPERTS = 32
TOPK = 4
SPLIT = 4
CAP = 10


norm_eps = 1e-06


def slot_numbers(routes):
    flat_routes = routes.reshape(routes.shape[:-2] + (-1,))
    matches = (flat_routes[..., None] == jnp.arange(EXPERTS, dtype=jnp.int32)).astype(jnp.int32)
    ranked = jnp.sum(matches * (jnp.cumsum(matches, axis=-2) - 1), axis=-1)
    return (flat_routes * CAP + ranked).reshape(routes.shape)


def attend_heads(queries, key_rows, value_rows, documents):
    score_scale = 1.0 / math.sqrt(queries.shape[-1])
    scores = (
        jnp.einsum("qhd,khd->hqk", queries, key_rows, preferred_element_type=jnp.float32)
        * score_scale
    )
    positions = jnp.arange(queries.shape[0], dtype=jnp.int32)
    allowed = (positions[:, None] >= positions[None, :]) & (
        documents[:, None] == documents[None, :]
    )
    scores = jnp.where(allowed[None], scores, -1e30)
    row_max = jnp.max(scores, axis=-1, keepdims=True)
    lifted = jnp.exp(scores - row_max)
    weights = (lifted / jnp.sum(lifted, axis=-1, keepdims=True)).astype(jnp.bfloat16)
    return jnp.einsum(
        "hqk,khd->qhd", weights, value_rows, preferred_element_type=jnp.float32
    ).astype(jnp.bfloat16)


def piece_block(row_block, gate_matrix, up_matrix, down_matrix):
    gate_act = jnp.einsum(
        "npcd,pdf->npcf", row_block, gate_matrix, preferred_element_type=jnp.float32
    )
    up_act = jnp.einsum("npcd,pdf->npcf", row_block, up_matrix, preferred_element_type=jnp.float32)
    hidden = (jax.nn.silu(gate_act) * up_act).astype(jnp.bfloat16)
    return jnp.einsum(
        "npcf,pfd->npcd", hidden, down_matrix, preferred_element_type=jnp.float32
    ).astype(jnp.bfloat16)


def shared_block(row_block, gate_matrix, up_matrix, down_matrix):
    gate_act = jnp.dot(row_block, gate_matrix, preferred_element_type=jnp.float32)
    up_act = jnp.dot(row_block, up_matrix, preferred_element_type=jnp.float32)
    hidden = (jax.nn.silu(gate_act) * up_act).astype(jnp.bfloat16)
    return jnp.dot(hidden, down_matrix, preferred_element_type=jnp.float32)


def body(
    resid,
    queries_keys,
    values,
    doc_ids,
    out_weight,
    norm_gain,
    expert_ids,
    gate_vals,
    expert_gate,
    expert_up,
    expert_down,
    shared_gate,
    shared_up,
    shared_down,
    shared_score,
):
    seq_count = lax.axis_size("seq")
    batch_count = lax.axis_size("dp")
    tokens = resid.shape[1]
    model_width = resid.shape[2]
    local_heads = model_width // HD // seq_count
    paired = queries_keys.reshape(2, tokens, seq_count, local_heads, HD)
    valued = values.reshape(1, tokens, seq_count, local_heads, HD)
    documents = doc_ids[0]
    pair_piece = lax.all_to_all(paired, "seq", split_axis=2, concat_axis=1, tiled=True)
    value_piece = lax.all_to_all(valued, "seq", split_axis=2, concat_axis=1, tiled=True)
    attended = attend_heads(
        pair_piece[0, :, 0], pair_piece[1, :, 0], value_piece[0, :, 0], documents
    )
    by_position = attended.reshape(seq_count, tokens, local_heads * HD)
    own_attended = lax.all_to_all(
        by_position, "seq", split_axis=0, concat_axis=2, tiled=True
    ).reshape(tokens, model_width)
    column_block = jnp.dot(
        lax.all_gather(own_attended, "dp", axis=0, tiled=True),
        out_weight,
        preferred_element_type=jnp.float32,
    ).astype(jnp.bfloat16)
    projected = lax.all_to_all(column_block, "dp", split_axis=0, concat_axis=1, tiled=True)
    residual = (resid[0].astype(jnp.float32) + projected.astype(jnp.float32)).astype(jnp.bfloat16)
    stream = residual.astype(jnp.float32)
    normed = (
        stream * lax.rsqrt(jnp.mean(stream * stream, axis=-1, keepdims=True) + norm_eps) * norm_gain
    ).astype(jnp.bfloat16)
    shared_parts = shared_block(
        lax.all_gather(normed, "dp", axis=0, tiled=True), shared_gate, shared_up, shared_down
    )
    shared_sum = lax.psum_scatter(
        shared_parts.astype(jnp.bfloat16), "dp", scatter_dimension=0, tiled=True
    ).astype(jnp.float32)
    share_weight = jax.nn.sigmoid(jnp.dot(normed, shared_score, preferred_element_type=jnp.float32))
    routes = expert_ids[0]
    route_gates = gate_vals[0]
    slot_ids = slot_numbers(routes)
    slot_range = jnp.arange(EXPERTS * CAP, dtype=jnp.int32)
    picked = jnp.sum(
        (slot_ids[None, :, :] == slot_range[:, None, None]).astype(jnp.int32), axis=-1
    ).astype(jnp.bfloat16)
    buffer = jnp.dot(picked, normed, preferred_element_type=jnp.float32).astype(jnp.bfloat16)
    outgoing = jnp.broadcast_to(
        buffer.reshape(EXPERTS, 1, CAP, model_width), (EXPERTS, SPLIT, CAP, model_width)
    )
    own_pieces = expert_gate.shape[0]
    devices = seq_count * batch_count
    incoming = lax.all_to_all(
        outgoing.reshape(EXPERTS * SPLIT, CAP, model_width),
        ("seq", "dp"),
        split_axis=0,
        concat_axis=0,
        tiled=True,
    )
    results = piece_block(
        incoming.reshape(devices, own_pieces, CAP, model_width), expert_gate, expert_up, expert_down
    )
    returned = lax.all_to_all(
        results.reshape(devices * own_pieces, CAP, model_width),
        ("seq", "dp"),
        split_axis=0,
        concat_axis=0,
        tiled=True,
    )
    expert_out = jnp.sum(
        returned.reshape(EXPERTS, SPLIT, CAP, model_width).astype(jnp.float32), axis=1
    ).reshape(EXPERTS * CAP, model_width)
    fetched = jnp.take(expert_out, slot_ids.reshape(-1), axis=0).reshape(tokens, TOPK, model_width)
    routed = jnp.sum(route_gates[..., None] * fetched, axis=1)
    layer_out = residual.astype(jnp.float32) + routed + share_weight[:, None] * shared_sum
    return layer_out.astype(jnp.bfloat16)[None]


def solution(mesh):
    placed = (
        P(("groups", "dp"), "seq", None),
        P(None, ("groups", "dp"), "seq", None),
        P(("groups", "dp"), "seq", None),
        P(("groups", "dp"), None),
        P(None, "dp"),
        P(),
        P(("groups", "dp"), "seq", None),
        P(("groups", "dp"), "seq", None),
        P(("seq", "dp"), None, None),
        P(("seq", "dp"), None, None),
        P(("seq", "dp"), None, None),
        P(None, "dp"),
        P(None, "dp"),
        P("dp", None),
        P(),
    )
    return jax.shard_map(
        body,
        mesh=mesh,
        in_specs=placed,
        out_specs=P(("groups", "dp"), "seq", None),
        check_vma=False,
    )
```

profile of v0, /device:TPU:0, one launch (start us, length us, event | category | flops | bytes accessed | tf_op | source)
XLA Modules:
  0.0 584.3 jit_solution(2189407843244324024)
XLA Ops:
  6.5 1.3 reshape.164
  7.8 0.8 copy.102
  8.6 4.3 all-to-all-start.1
  12.9 1.4 reshape.163
  14.3 0.9 copy.99
  15.2 4.2 all-to-all-done.1
  19.4 3.5 all-to-all-start
  22.9 0.0 all-gather.3.cloned.1.call-start
  22.9 0.1 fusion.41
  23.0 1.7 copy.103
  24.7 6.9 %all-to-all-done = bf16[2,64,4,4,128]{4,1,3,0,2:T(8,128)(2,1)S(1)} async-done(((bf16[2,64,4,4,128]{4,1,3,0,2:T(8,128)(2,1)}), bf16[2,64,4,4,128]{4,1,3,0,2:T(8,128)(2,1)S(1)}, u32[]{:S(2)}, u32[]{:S(2)}) %all-to-all-start) | async-done | bytes 524320 | tf_op jit(solution)/shard_map/all_to_all | solution.py:87
  31.7 1.3 fusion.21
  33.0 0.5 fusion.53
  33.5 2.1 fusion.27
  35.7 0.2 copy.105
  35.9 0.1 reshape.165
  36.0 8.4 %all_to_all.68 = bf16[4,64,512]{2,1,0:T(8,128)(2,1)S(1)} all-to-all(bf16[4,64,512]{2,1,0:T(8,128)(2,1)S(1)} %reshape.165), channel_id=1, replica_groups=mesh['groups'=2,'seq'=4,'dp'=4] {'seq'}, dimensions={0} | all-to-all | bytes 524288 | tf_op jit(solution)/shard_map/all_to_all | solution.py:93
  44.4 0.2 copy.106
  44.6 0.8 copy.132
  45.3 0.0 all-gather.3.cloned.1.call-update
  45.4 0.1 copy.109
  45.5 0.1 eq.64
  45.6 0.1 reshape_squeeze.3
  45.7 0.6 reduce-window.6
  46.3 0.2 slice_reduce_fusion
  46.5 28.1 %all-gather.3.cloned.1.call-done = bf16[256,2048]{1,0:T(8,128)(2,1)} async-done(((bf16[64,2048]{1,0:T(8,128)(2,1)}), bf16[256,2048]{1,0:T(8,128)(2,1)}) %all-gather.3.cloned.1.call-update) | async-done | bytes 1048592 | tf_op jit(solution)/shard_map/all_gather | solution.py:97
  74.6 3.3 convolution_convert_fusion.2
  77.9 3.4 all-to-all-start.3
  81.3 0.1 fusion.44
  81.4 0.1 reduce_sum.63
  81.5 0.1 copy.114
  81.6 0.1 convert_reduce_fusion.1
  81.8 8.2 %all-to-all-done.3 = bf16[4,64,512]{2,1,0:T(8,128)(2,1)S(1)} async-done(((bf16[4,64,512]{2,1,0:T(8,128)(2,1)}), bf16[4,64,512]{2,1,0:T(8,128)(2,1)S(1)}, u32[]{:S(2)}, u32[]{:S(2)}) %all-to-all-start.3) | async-done | bytes 262176 | tf_op jit(solution)/shard_map/all_to_all | solution.py:101
  90.1 1.1 fusion.33
  91.2 0.1 fusion.35
  91.4 1.6 convolution_convert_fusion
  93.0 3.3 broadcast_in_dim.45
  96.3 2.6 broadcast_in_dim.46
  99.0 188.0 %all_to_all.69 = bf16[128,10,2048]{2,1,0:T(8,128)(2,1)} all-to-all(bf16[128,10,2048]{2,1,0:T(8,128)(2,1)S(1)} %bitcast.137), channel_id=1, replica_groups=mesh['groups'=2,'seq'=4,'dp'=4] {'seq','dp'}, dimensions={0} | all-to-all | bytes 10485760 | tf_op jit(solution)/shard_map/all_to_all | solution.py:127
  286.9 12.4 %fusion.5 = f32[8,16,10,352]{3,1,2,0:T(8,128)} fusion(bf16[8,2048,352]{1,2,0:T(8,128)(2,1)} %param.23, bf16[16,8,10,2048]{3,2,1,0:T(8,128)(2,1)} %bitcast.139), kind=kOutput, calls=%fused_computation.7 | convolution fusion | flops 1845493760 | bytes 18579456 | tf_op jit(solution)/shard_map/npcd,pdf->npcf/dot_general | solution.py:45
  299.4 16.0 %convert_bitcast_fusion = bf16[16,8,10,2048]{3,0,2,1:T(8,128)(2,1)} fusion(bf16[8,352,2048]{2,1,0:T(8,128)(2,1)} %param.25, f32[8,16,10,352]{3,1,2,0:T(8,128)} %fusion.5, bf16[8,2048,352]{1,2,0:T(8,128)(2,1)} %param.24, bf16[16,8,10,2048]{3,2,1,0:T(8,128)(2,1)} %bitcast.140), kind=kOutput, calls=%fused_computation.10 | convolution fusion | flops 3696312320 | bytes 35356672 | tf_op jit(solution)/shard_map/npcf,pfd->npcd/dot_general | solution.py:50
  315.3 6.0 %copy.143 = bf16[16,8,10,2048]{3,1,0,2:T(8,128)(2,1)S(1)} copy(bf16[16,8,10,2048]{3,0,2,1:T(8,128)(2,1)} %convert_bitcast_fusion) | data formatting | bytes 10485760 | tf_op jit(solution)/shard_map/convert_element_type | solution.py:52
  321.4 6.5 %copy.119 = bf16[128,10,2048]{2,1,0:T(8,128)(2,1)} copy(bf16[128,10,2048]{2,0,1:T(8,128)(2,1)S(1)} %bitcast.138) | data formatting | bytes 10485760 | tf_op jit(solution)/shard_map/reshape | solution.py:138
  327.9 4.7 all-to-all-start.5
  332.6 0.0 all-gather.5.cloned.1.call-start
  332.7 0.7 all-gather.5.cloned.1.call-update
  333.4 0.3 reduce-scatter.2.cloned.1.call-start
  333.7 74.4 %all-gather.5.cloned.1.call-done = bf16[256,2048]{1,0:T(8,128)(2,1)} async-done(((bf16[64,2048]{1,0:T(8,128)(2,1)}), bf16[256,2048]{1,0:T(8,128)(2,1)}) %all-gather.5.cloned.1.call-update) | async-done | bytes 1048592 | tf_op jit(solution)/shard_map/all_gather | solution.py:108
  408.1 4.0 fusion.54
  412.1 6.6 %convolution_convert_fusion.1 = bf16[256,2048]{1,0:T(8,128)(2,1)} fusion(bf16[704,2048]{1,0:T(8,128)(2,1)S(1)} %copy-done, bf16[256,2048]{1,0:T(8,128)(2,1)} %all-gather.5.cloned.1.call-done, bf16[2048,704]{0,1:T(8,128)(2,1)} %param.27, f32[256,704]{0,1:T(8,128)} %fusion.54), kind=kOutput, calls=%fused_computation.14 | convolution fusion | flops 1478000640 | bytes 8585216 | tf_op jit(solution)/shard_map/dot_general | solution.py:59
  418.7 0.1 reduce_sum.62
  418.8 0.1 copy.122
  418.9 0.1 mul.98
  419.0 0.1 copy.112
  419.1 0.1 copy.113
  419.2 0.1 copy.108
  419.4 0.2 fusion.31
  419.6 130.9 %all-to-all-done.5 = bf16[128,10,2048]{2,1,0:T(8,128)(2,1)} async-done(((bf16[128,10,2048]{2,1,0:T(8,128)(2,1)}), bf16[128,10,2048]{2,1,0:T(8,128)(2,1)}, u32[]{:S(2)}, u32[]{:S(2)}) %all-to-all-start.5) | async-done | bytes 5242912 | tf_op jit(solution)/shard_map/all_to_all | solution.py:137
  550.5 7.8 %convert_reduce_fusion = f32[32,10,2048]{2,1,0:T(8,128)} fusion(bf16[128,10,2048]{2,1,0:T(8,128)(2,1)} %all-to-all-done.5), kind=kLoop, calls=%fused_computation.2 | loop fusion | flops 4587520 | bytes 7864320 | tf_op jit(solution)/shard_map/reduce_sum | solution.py:144
  558.3 4.5 reshape.171
  562.8 5.3 gather_fusion
  568.2 2.9 gather.7
  571.0 4.7 multiply_reduce_fusion
  575.8 2.0 fusion.40
  (32 shorter events, 0.3 us)
Async XLA Ops:
  6.5 405.5 %copy-start = (bf16[704,2048]{1,0:T(8,128)(2,1)S(1)}, bf16[704,2048]{1,0:T(8,128)(2,1)}, u32[]{:S(2)}) copy-start(bf16[704,2048]{1,0:T(8,128)(2,1)} %param.28) | copy-start | bytes 8650756
  6.5 16.4 %copy-start.6 = (s32[1,256]{1,0:T(1,128)S(1)}, s32[1,256]{1,0:T(1,128)}, u32[]{:S(2)}) copy-start(s32[1,256]{1,0:T(1,128)} %param.18) | copy-start | bytes 3076
  8.6 10.8 %all-to-all-start.1 = ((bf16[1,64,4,4,128]{4,1,3,0,2:T(8,128)(2,1)}), bf16[1,64,4,4,128]{4,1,3,0,2:T(8,128)(2,1)}, u32[]{:S(2)}, u32[]{:S(2)}) async-start(bf16[1,64,4,4,128]{4,1,3,0,2:T(8,128)(2,1)} %copy.102), calls=%async_computation.1 | async-start | bytes 524288 | tf_op jit(solution)/shard_map/all_to_all | solution.py:88
  19.4 12.3 %all-to-all-start = ((bf16[2,64,4,4,128]{4,1,3,0,2:T(8,128)(2,1)}), bf16[2,64,4,4,128]{4,1,3,0,2:T(8,128)(2,1)S(1)}, u32[]{:S(2)}, u32[]{:S(2)}) async-start(bf16[2,64,4,4,128]{4,1,3,0,2:T(8,128)(2,1)} %copy.99), calls=%async_computation | async-start | bytes 1048576 | tf_op jit(solution)/shard_map/all_to_all | solution.py:87
  22.9 51.7 %all-gather.3.cloned.1.call-start = ((), (), s32[]{:S(2)}) async-start(), calls=%async_computation.7 | async-start | bytes 1310720 | tf_op jit(solution)/shard_map/all_gather | solution.py:97
  33.5 11.8 %copy-start.3 = (s32[1,64,4]{1,2,0:T(4,128)S(1)}, s32[1,64,4]{1,2,0:T(4,128)}, u32[]{:S(2)}) copy-start(s32[1,64,4]{1,2,0:T(4,128)} %param.21) | copy-start | bytes 3076
  46.5 44.7 %copy-start.4 = (f32[2048]{0:T(1024)S(1)}, f32[2048]{0:T(1024)}, u32[]{:S(2)}) copy-start(f32[2048]{0:T(1024)} %param.20) | copy-start | bytes 24580
  77.9 12.1 %all-to-all-start.3 = ((bf16[4,64,512]{2,1,0:T(8,128)(2,1)}), bf16[4,64,512]{2,1,0:T(8,128)(2,1)S(1)}, u32[]{:S(2)}, u32[]{:S(2)}) async-start(bf16[4,64,512]{2,1,0:T(8,128)(2,1)} %bitcast.13), calls=%async_computation.3 | async-start | bytes 524288 | tf_op jit(solution)/shard_map/all_to_all | solution.py:101
  91.4 7.6 %copy-start.1 = (bf16[64,2048]{1,0:T(8,128)(2,1)}, bf16[64,2048]{1,0:T(8,128)(2,1)S(1)}, u32[]{:S(2)}) copy-start(bf16[64,2048]{1,0:T(8,128)(2,1)S(1)} %fusion.35) | copy-start | bytes 786436
  327.9 222.6 %all-to-all-start.5 = ((bf16[128,10,2048]{2,1,0:T(8,128)(2,1)}), bf16[128,10,2048]{2,1,0:T(8,128)(2,1)}, u32[]{:S(2)}, u32[]{:S(2)}) async-start(bf16[128,10,2048]{2,1,0:T(8,128)(2,1)} %copy.119), calls=%async_computation.5 | async-start | bytes 16777216 | tf_op jit(solution)/shard_map/all_to_all | solution.py:137
  332.6 75.4 %all-gather.5.cloned.1.call-start = ((), (), s32[]{:S(2)}) async-start(), calls=%async_computation.8 | async-start | bytes 1310720 | tf_op jit(solution)/shard_map/all_gather | solution.py:108
  333.4 242.4 %reduce-scatter.2.cloned.1.call-start = ((), (), s32[]{:S(2)}) async-start(), calls=%async_computation.9 | async-start | bytes 1310720 | tf_op jit(solution)/shard_map/reduce_scatter | solution.py:110
  412.0 7.2 %copy-start.7 = (f32[1,64,4]{1,2,0:T(4,128)S(1)}, f32[1,64,4]{1,2,0:T(4,128)}, u32[]{:S(2)}) copy-start(f32[1,64,4]{1,2,0:T(4,128)} %param.22) | copy-start | bytes 3076
  412.0 7.3 %copy-start.5 = (bf16[2048]{0:T(1024)(128)(2,1)S(1)}, bf16[2048]{0:T(1024)(128)(2,1)}, u32[]{:S(2)}) copy-start(bf16[2048]{0:T(1024)(128)(2,1)} %param.29) | copy-start | bytes 12292
  412.1 7.3 %copy-start.2 = (bf16[64,2048]{1,0:T(8,128)(2,1)S(1)}, bf16[64,2048]{1,0:T(8,128)(2,1)}, u32[]{:S(2)}) copy-start(bf16[64,2048]{1,0:T(8,128)(2,1)} %copy-done.1) | copy-start | bytes 786436
Sparse Core Ops, SparseCore 0:
  45.5 29.0 all-gather.2
  335.0 73.0 all-gather.4
  418.8 73.1 reduce-scatter.1
where the time goes:
time: 585 us; the launch traced here: 584 us
  waiting for transfers between devices  253 us (43%)
  blocking collectives  196 us (34%)
  matrix products  48 us (8%)
  local copies, waits for them, and re-layouts  40 us (7%)
  other arithmetic  16.8 us (3%)
  starting transfers between devices  16.3 us (3%)
  between operations  13.4 us (2%)
    all_to_all x1, blocking collectives, body(): lax.all_to_all(outgoing.reshape(EXPERTS * SPLIT, CAP, model_width), ('seq...  188 us
    all_to_all x1, waiting for transfers between devices, body(): lax.all_to_all(results.reshape(devices * own_pieces, CAP, model_width), (...  131 us
    all_gather x1, waiting for transfers between devices, body(): lax.all_gather(normed, 'dp', axis=0, tiled=True)  74.4 us
    all_gather x1, waiting for transfers between devices, body(): lax.all_gather(own_attended, 'dp', axis=0, tiled=True)  28.1 us
    dot_general x1, matrix products, piece_block(): jnp.einsum('npcf,pfd->npcd', hidden, down_matrix, preferred_element_type=...  16 us
    dot_general x1, matrix products, piece_block(): jnp.einsum('npcd,pdf->npcf', row_block, gate_matrix, preferred_element_ty...  12.4 us
  transfers between devices with their start and end apart: 7, of which 6 were waited for; matrix products, arithmetic and copies ran while one was open for 7% of the time, Pallas kernels for 0%

commit v1 on v0

--- a/solution.py
+++ b/solution.py
@@ -57,6 +57,59 @@
     up_act = jnp.dot(row_block, up_matrix, preferred_element_type=jnp.float32)
     hidden = (jax.nn.silu(gate_act) * up_act).astype(jnp.bfloat16)
     return jnp.dot(hidden, down_matrix, preferred_element_type=jnp.float32)
+
+
+def gathered_layer(residual, normed, expert_ids, gate_vals, gate, up, down, shared, score):
+    everyone = ("seq", "dp")
+    seq_count, batch_count = lax.axis_size("seq"), lax.axis_size("dp")
+    devices = seq_count * batch_count
+    tokens, width = normed.shape
+    own_experts = gate.shape[0] // SPLIT
+    room = devices * CAP
+    table = jnp.concatenate([expert_ids[0].astype(jnp.float32), gate_vals[0]], axis=1)
+    table = lax.all_gather(table, everyone, axis=0, tiled=True)
+    me = lax.axis_index("seq") * batch_count + lax.axis_index("dp")
+    mine = (me * own_experts + jnp.arange(own_experts)).astype(jnp.float32)
+    named = (table[:, :TOPK, None] == mine).astype(jnp.float32)
+    weight = jnp.sum(named * table[:, TOPK:, None], axis=1)
+    named = jnp.sum(named, axis=1)
+    total = devices * tokens
+    order = jnp.arange(total)
+    before = (order[None, :] < order[:, None]).astype(jnp.bfloat16)
+    rank = jnp.dot(before, named.astype(jnp.bfloat16), preferred_element_type=jnp.float32)
+    spot = jnp.where(named > 0, rank, -1.0)
+    pick = spot.T[:, None, :] == jnp.arange(room, dtype=jnp.float32)[None, :, None]
+    slot_gate = jnp.sum(jnp.where(pick, weight.T[:, None, :], 0.0), axis=-1)
+    pick = pick.astype(jnp.bfloat16).reshape(own_experts * room, total)
+
+    pool = lax.all_gather(normed, everyone, axis=0, tiled=True)
+    rows = jnp.dot(pick, pool, preferred_element_type=jnp.float32).astype(jnp.bfloat16)
+    rows = rows.reshape(own_experts, room, width)
+    gate = gate.reshape((own_experts, SPLIT) + gate.shape[1:])
+    up = up.reshape((own_experts, SPLIT) + up.shape[1:])
+    down = down.reshape((own_experts, SPLIT) + down.shape[1:])
+    gate_act = jnp.einsum("ecd,ebdf->ebcf", rows, gate, preferred_element_type=jnp.float32)
+    up_act = jnp.einsum("ecd,ebdf->ebcf", rows, up, preferred_element_type=jnp.float32)
+    hidden = (jax.nn.silu(gate_act) * up_act).astype(jnp.bfloat16)
+    expert_out = jnp.einsum("ebcf,ebfd->ecd", hidden, down, preferred_element_type=jnp.float32)
+    expert_out = (expert_out * slot_gate[..., None]).astype(jnp.bfloat16)
+    partial = lax.dot_general(
+        pick,
+        expert_out.reshape(own_experts * room, width),
+        (((0,), (0,)), ((), ())),
+        preferred_element_type=jnp.float32,
+    ).reshape(seq_count, batch_count * tokens, width)
+    s = lax.axis_index("seq")
+    line = lax.dynamic_slice_in_dim(pool, s * batch_count * tokens, batch_count * tokens)
+    share_weight = jax.nn.sigmoid(jnp.dot(line, score, preferred_element_type=jnp.float32))
+    shared_part = shared_block(line, *shared) * share_weight[:, None]
+    here = (jnp.arange(seq_count) == s)[:, None, None]
+    partial = jnp.where(here, partial + shared_part[None], partial).astype(jnp.bfloat16)
+    summed = lax.psum_scatter(
+        partial.reshape(total, width), everyone, scatter_dimension=0, tiled=True
+    )
+    out = residual.astype(jnp.float32) + summed.astype(jnp.float32)
+    return out.astype(jnp.bfloat16)[None]
 
 
 def body(
@@ -104,6 +157,18 @@
     normed = (
         stream * lax.rsqrt(jnp.mean(stream * stream, axis=-1, keepdims=True) + norm_eps) * norm_gain
     ).astype(jnp.bfloat16)
+    if expert_gate.shape[0] % SPLIT == 0:
+        return gathered_layer(
+            residual,
+            normed,
+            expert_ids,
+            gate_vals,
+            expert_gate,
+            expert_up,
+            expert_down,
+            (shared_gate, shared_up, shared_down),
+            shared_score,
+        )
     shared_parts = shared_block(
         lax.all_gather(normed, "dp", axis=0, tiled=True), shared_gate, shared_up, shared_down
     )

time: 585 us -> 265 us (0.45)
  blocking collectives: 196 us -> 51.1 us
  waiting for transfers between devices: 253 us -> 130 us
  local copies, waits for them, and re-layouts: 40 us -> 7.67 us
  other arithmetic: 16.8 us -> 3.54 us
  starting transfers between devices: 16.3 us -> 7.86 us
    all_to_all x1, blocking collectives: 188 us -> 11.7 us  [body(): lax.all_to_all(column_block, 'dp', split_axis=0, concat_axis=1, tiled=True)]
    all_to_all x2 -> x0, waiting for transfers between devices: 139 us -> none  [the longest x1 131 us: body(): lax.all_to_all(results.reshape(devices * own_pieces, CAP, model_width), (...]
    reduce_scatter x1, waiting for transfers between devices: 0.01 us -> 71.3 us  [gathered_layer(): lax.psum_scatter(partial.reshape(total, width), everyone, scatter_dimensi...]
    all_gather x1, waiting for transfers between devices: 74.4 us -> 18 us  [gathered_layer(): pool = lax.all_gather(normed, everyone, axis=0, tiled=True)]
    all_gather x0 -> x1, blocking collectives: none -> 31 us  [gathered_layer(): table = lax.all_gather(table, everyone, axis=0, tiled=True)]
    reduce_sum x4 -> x2, other arithmetic: 12.8 us -> 0.35 us  [the longest x1 0.23 us: gathered_layer(): slot_gate = jnp.sum(jnp.where(pick, weight.T[:, None, :], 0.0), axis=-1)]
    reshape x2 -> x0, local copies, waits for them, and re-layouts: 11 us -> none  [the longest x1 6.52 us: body(): results.reshape(devices * own_pieces, CAP, model_width)]
    gather x2 -> x0, local copies, waits for them, and re-layouts: 8.21 us -> none  [body(): jnp.take(expert_out, slot_ids.reshape(-1), axis=0)]
  transfers between devices with their start and end apart: 7 -> 5, of which waited for: 6 -> 5; matrix products, arithmetic and copies ran while one was open for 7% -> 2% of each run, Pallas kernels for 0% -> 0%
where the time goes in v1:
time: 265 us
  waiting for transfers between devices  130 us (49%)
  matrix products  51.4 us (19%)
  blocking collectives  51.1 us (19%)
  between operations  13.4 us (5%)
  starting transfers between devices  7.86 us (3%)
  local copies, waits for them, and re-layouts  7.67 us (3%)
  other arithmetic  3.54 us (1%)
    reduce_scatter x1, waiting for transfers between devices, gathered_layer(): lax.psum_scatter(partial.reshape(total, width), everyone, scatter_dimensi...  71.3 us
    all_gather x1, blocking collectives, gathered_layer(): table = lax.all_gather(table, everyone, axis=0, tiled=True)  31 us
    all_gather x1, waiting for transfers between devices, body(): lax.all_gather(own_attended, 'dp', axis=0, tiled=True)  29.2 us
    all_gather x1, waiting for transfers between devices, gathered_layer(): pool = lax.all_gather(normed, everyone, axis=0, tiled=True)  18 us
    all_to_all x1, blocking collectives, body(): lax.all_to_all(column_block, 'dp', split_axis=0, concat_axis=1, tiled=True)  11.7 us
    all_to_all x1, blocking collectives, body(): lax.all_to_all(by_position, 'seq', split_axis=0, concat_axis=2, tiled=True)  8.39 us
    dot_general x1, matrix products, gathered_layer(): jnp.einsum('ecd,ebdf->ebcf', rows, up, preferred_element_type=jnp.float32)  8.18 us
    dot_general x1, matrix products, gathered_layer(): jnp.einsum('ebcf,ebfd->ecd', hidden, down, preferred_element_type=jnp.flo...  7.73 us
  transfers between devices with their start and end apart: 5, of which 5 were waited for; matrix products, arithmetic and copies ran while one was open for 2% of the time, Pallas kernels for 0%

profile of v1, /device:TPU:0, one launch (start us, length us, event | category | flops | bytes accessed | tf_op | source)
XLA Modules:
  0.0 264.5 jit_solution(17314013647062686856)
XLA Ops:
  6.5 0.0 copy-start
  6.5 0.0 copy-start.4
  6.5 1.3 reshape.120
  7.8 0.8 copy.57
  8.6 4.3 %all-to-all-start.1 = ((bf16[1,64,4,4,128]{4,1,3,0,2:T(8,128)(2,1)}), bf16[1,64,4,4,128]{4,1,3,0,2:T(8,128)(2,1)}, u32[]{:S(2)}, u32[]{:S(2)}) async-start(bf16[1,64,4,4,128]{4,1,3,0,2:T(8,128)(2,1)} %copy.57), calls=%async_computation.1 | async-start | bytes 524288 | tf_op jit(solution)/shard_map/all_to_all | solution.py:141
  12.9 1.4 reshape.119
  14.3 0.9 copy.54
  15.2 4.2 %all-to-all-done.1 = bf16[1,64,4,4,128]{4,1,3,0,2:T(8,128)(2,1)} async-done(((bf16[1,64,4,4,128]{4,1,3,0,2:T(8,128)(2,1)}), bf16[1,64,4,4,128]{4,1,3,0,2:T(8,128)(2,1)}, u32[]{:S(2)}, u32[]{:S(2)}) %all-to-all-start.1) | async-done | bytes 262176 | tf_op jit(solution)/shard_map/all_to_all | solution.py:141
  19.4 3.5 %all-to-all-start = ((bf16[2,64,4,4,128]{4,1,3,0,2:T(8,128)(2,1)}), bf16[2,64,4,4,128]{4,1,3,0,2:T(8,128)(2,1)S(1)}, u32[]{:S(2)}, u32[]{:S(2)}) async-start(bf16[2,64,4,4,128]{4,1,3,0,2:T(8,128)(2,1)} %copy.54), calls=%async_computation | async-start | bytes 1048576 | tf_op jit(solution)/shard_map/all_to_all | solution.py:140
  22.9 0.0 all-gather.4.cloned.1.call-start
  22.9 0.0 copy-done.4
  22.9 0.1 fusion.36
  23.0 1.7 copy.58
  24.7 6.9 %all-to-all-done = bf16[2,64,4,4,128]{4,1,3,0,2:T(8,128)(2,1)S(1)} async-done(((bf16[2,64,4,4,128]{4,1,3,0,2:T(8,128)(2,1)}), bf16[2,64,4,4,128]{4,1,3,0,2:T(8,128)(2,1)S(1)}, u32[]{:S(2)}, u32[]{:S(2)}) %all-to-all-start) | async-done | bytes 524320 | tf_op jit(solution)/shard_map/all_to_all | solution.py:140
  31.7 1.3 fusion.11
  33.0 0.5 fusion.51
  33.5 2.1 fusion.15
  35.7 0.2 copy.60
  35.9 0.1 reshape.121
  36.0 8.4 %all_to_all.58 = bf16[4,64,512]{2,1,0:T(8,128)(2,1)S(1)} all-to-all(bf16[4,64,512]{2,1,0:T(8,128)(2,1)S(1)} %reshape.121), channel_id=1, replica_groups=mesh['groups'=2,'seq'=4,'dp'=4] {'seq'}, dimensions={0} | all-to-all | bytes 524288 | tf_op jit(solution)/shard_map/all_to_all | solution.py:146
  44.4 0.2 copy.61
  44.6 0.8 copy.70
  45.3 0.0 all-gather.4.cloned.1.call-update
  45.4 0.0 copy-start.1
  45.4 0.0 all-gather.6.cloned.1.call-start
  45.4 29.2 %all-gather.4.cloned.1.call-done = bf16[256,2048]{1,0:T(8,128)(2,1)} async-done(((bf16[64,2048]{1,0:T(8,128)(2,1)}), bf16[256,2048]{1,0:T(8,128)(2,1)}) %all-gather.4.cloned.1.call-update) | async-done | bytes 1048592 | tf_op jit(solution)/shard_map/all_gather | solution.py:150
  74.6 2.6 convolution_convert_fusion.1
  77.2 0.0 copy-start.2
  77.2 0.0 copy-start.3
  77.2 0.0 copy-start.5
  77.2 0.0 copy-start.6
  77.3 11.7 %all_to_all.59 = bf16[4,64,512]{2,1,0:T(8,128)(2,1)S(1)} all-to-all(bf16[4,64,512]{2,1,0:T(8,128)(2,1)S(1)} %bitcast.121), channel_id=1, replica_groups=mesh['groups'=2,'seq'=4,'dp'=4] {'dp'}, dimensions={0} | all-to-all | bytes 524288 | tf_op jit(solution)/shard_map/all_to_all | solution.py:154
  89.1 0.0 copy-done.1
  89.1 0.2 fusion.29
  89.3 0.0 copy-done.2
  89.3 0.8 fusion.31
  90.1 0.0 all-gather.6.cloned.1.call-update
  90.2 0.0 reduce-scatter.2.cloned.1.call-start
  90.2 0.0 copy-done.3
  90.2 0.0 copy-done.5
  90.3 0.0 copy-done.6
  90.3 31.0 %all-gather = f32[16,64,8]{1,2,0:T(8,128)S(1)} all-gather(f32[1,64,8]{1,2,0:T(8,128)S(1)} %maximum_bitcast_fusion), channel_id=1, replica_groups=mesh['groups'=2,'seq'=4,'dp'=4] {'seq','dp'}, dimensions={0}, use_global_device_ids=true | all-gather | bytes 34816 | tf_op jit(solution)/shard_map/all_gather | solution.py:70
  121.3 0.1 reshape.132
  121.4 0.1 eq.78
  121.5 0.1 fusion.38
  121.6 0.5 fusion.16
  122.0 0.3 bitcast_compare_fusion
  122.3 0.2 select_reduce_fusion
  122.6 18.0 %all-gather.6.cloned.1.call-done = bf16[1024,2048]{1,0:T(8,128)(2,1)} async-done(((bf16[64,2048]{1,0:T(8,128)(2,1)}), bf16[1024,2048]{1,0:T(8,128)(2,1)}) %all-gather.6.cloned.1.call-update) | async-done | bytes 4194320 | tf_op jit(solution)/shard_map/all_gather | solution.py:85
  140.6 1.6 fusion.17
  142.2 3.7 %convolution_convert_fusion = bf16[320,2048]{1,0:T(8,128)(2,1)S(1)} fusion(pred[320,1024]{1,0:T(8,128)(4,1)S(1)} %bitcast_compare_fusion, bf16[1024,2048]{1,0:T(8,128)(2,1)} %all-gather.6.cloned.1.call-done), kind=kOutput, calls=%fused_computation.9 | convolution fusion | flops 1342832640 | bytes 5832704 | tf_op jit(solution)/shard_map/dot_general | solution.py:86
  145.9 6.9 %fusion.52 = f32[2,160,4,352]{3,1,2,0:T(8,128)S(1)} fusion(bf16[2,160,2048,1]{2,1,3,0:T(8,128)(2,1)S(1)} %bitcast.110, bf16[2,4,2048,352]{2,3,1,0:T(8,128)(2,1)} %bitcast.106), kind=kOutput, calls=%fused_computation.78 | convolution fusion | flops 1845493760 | bytes 14647296 | tf_op jit(solution)/shard_map/ecd,ebdf->ebcf/dot_general | solution.py:91
  152.8 8.2 %fusion.5 = bf16[2,4,160,352]{3,2,1,0:T(8,128)(2,1)S(1)} fusion(f32[2,160,4,352]{3,1,2,0:T(8,128)S(1)} %fusion.52, bf16[2,160,2048,1]{2,1,3,0:T(8,128)(2,1)S(1)} %bitcast.111, bf16[2,4,2048,352]{2,3,1,0:T(8,128)(2,1)} %bitcast.126), kind=kOutput, calls=%fused_computation.11 | convolution fusion | flops 1848197120 | bytes 15548416 | tf_op jit(solution)/shard_map/ecd,ebdf->ebcf/dot_general | solution.py:92
  161.0 0.0 copy-start.7
  161.0 7.7 %fusion.4 = bf16[2,160,2048]{2,1,0:T(8,128)(2,1)} fusion(bf16[2,4,160,352]{3,2,1,0:T(8,128)(2,1)S(1)} %fusion.5, bf16[2,4,352,2048]{3,2,1,0:T(8,128)(2,1)} %bitcast.127, f32[2,160]{1,0:T(2,128)S(1)} %select_reduce_fusion), kind=kOutput, calls=%fused_computation.8 | convolution fusion | flops 1846804480 | bytes 13747456 | tf_op jit(solution)/shard_map/ebcf,ebfd->ecd/dot_general | solution.py:94
  168.7 0.0 copy-done.7
  168.7 3.1 %fusion.20 = f32[256,704]{0,1:T(8,128)} fusion(bf16[2048,704]{0,1:T(8,128)(2,1)S(1)} %copy-done.7, bf16[1024,2048]{1,0:T(8,128)(2,1)} %all-gather.6.cloned.1.call-done, s32[]{:T(128)S(6)} %select_n.23), kind=kOutput, calls=%fused_computation.36 | convolution fusion | flops 738197504 | bytes 4653060 | tf_op jit(solution)/shard_map/dot_general | solution.py:56
  171.8 0.0 copy-done
  171.8 6.9 %convolution_multiply_fusion = f32[256,2048]{1,0:T(8,128)} fusion(bf16[704,2048]{1,0:T(8,128)(2,1)S(1)} %copy-done, f32[256]{0:T(256)S(1)} %add_divide_fusion, bf16[2048,704]{0,1:T(8,128)(2,1)} %param.27, bf16[1024,2048]{1,0:T(8,128)(2,1)} %all-gather.6.cloned.1.call-done, s32[]{:T(128)S(6)} %select_n.23, f32[256,704]{0,1:T(8,128)} %fusion.20), kind=kOutput, calls=%fused_computation.7 | convolution fusion | flops 1478000640 | bytes 9634820 | tf_op jit(solution)/shard_map/dot_general | solution.py:59
  178.7 6.3 %fusion.1 = bf16[4,256,2048]{2,1,0:T(8,128)(2,1)} fusion(f32[256,2048]{1,0:T(8,128)} %convolution_multiply_fusion, pred[4]{0:T(512)(128)(4,1)S(1)} %iota_compare_fusion.6, bf16[320,2048,1]{1,0,2:T(8,128)(2,1)} %bitcast.128, pred[40,4,8,256]{3,2,1,0:T(8,128)(4,1)S(1)} %bitcast.119), kind=kOutput, calls=%fused_computation.2 | convolution fusion | flops 1348468736 | bytes 7929860 | tf_op jit(solution)/shard_map/dot_general | solution.py:96
  185.0 0.0 reduce-scatter.2.cloned.1.call-update
  185.0 71.3 %reduce-scatter.2.cloned.1.call-done = bf16[64,2048]{1,0:T(8,128)(2,1)} async-done(((bf16[1024,2048]{1,0:T(8,128)(2,1)}), bf16[64,2048]{1,0:T(8,128)(2,1)}) %reduce-scatter.2.cloned.1.call-update) | async-done | bytes 262160 | tf_op jit(solution)/shard_map/reduce_scatter | solution.py:108
  256.3 1.7 fusion.35
  (15 shorter events, 0.2 us)
Async XLA Ops:
  6.5 165.2 %copy-start = (bf16[704,2048]{1,0:T(8,128)(2,1)S(1)}, bf16[704,2048]{1,0:T(8,128)(2,1)}, u32[]{:S(2)}) copy-start(bf16[704,2048]{1,0:T(8,128)(2,1)} %param.28) | copy-start | bytes 8650756
  6.5 16.4 %copy-start.4 = (s32[1,256]{1,0:T(1,128)S(1)}, s32[1,256]{1,0:T(1,128)}, u32[]{:S(2)}) copy-start(s32[1,256]{1,0:T(1,128)} %param.18) | copy-start | bytes 3076
  8.6 10.8 %all-to-all-start.1 = ((bf16[1,64,4,4,128]{4,1,3,0,2:T(8,128)(2,1)}), bf16[1,64,4,4,128]{4,1,3,0,2:T(8,128)(2,1)}, u32[]{:S(2)}, u32[]{:S(2)}) async-start(bf16[1,64,4,4,128]{4,1,3,0,2:T(8,128)(2,1)} %copy.57), calls=%async_computation.1 | async-start | bytes 524288 | tf_op jit(solution)/shard_map/all_to_all | solution.py:141
  19.4 12.3 %all-to-all-start = ((bf16[2,64,4,4,128]{4,1,3,0,2:T(8,128)(2,1)}), bf16[2,64,4,4,128]{4,1,3,0,2:T(8,128)(2,1)S(1)}, u32[]{:S(2)}, u32[]{:S(2)}) async-start(bf16[2,64,4,4,128]{4,1,3,0,2:T(8,128)(2,1)} %copy.54), calls=%async_computation | async-start | bytes 1048576 | tf_op jit(solution)/shard_map/all_to_all | solution.py:140
  22.9 51.7 %all-gather.4.cloned.1.call-start = ((), (), s32[]{:S(2)}) async-start(), calls=%async_computation.5 | async-start | bytes 1310720 | tf_op jit(solution)/shard_map/all_gather | solution.py:150
  45.4 43.7 %copy-start.1 = (bf16[1,64,2048]{2,1,0:T(8,128)(2,1)S(1)}, bf16[1,64,2048]{2,1,0:T(8,128)(2,1)}, u32[]{:S(2)}) copy-start(bf16[1,64,2048]{2,1,0:T(8,128)(2,1)} %param.15) | copy-start | bytes 786436
  45.4 95.2 %all-gather.6.cloned.1.call-start = ((), (), s32[]{:S(2)}) async-start(), calls=%async_computation.6 | async-start | bytes 4456448 | tf_op jit(solution)/shard_map/all_gather | solution.py:85
  77.2 12.1 %copy-start.2 = (f32[2048]{0:T(1024)S(1)}, f32[2048]{0:T(1024)}, u32[]{:S(2)}) copy-start(f32[2048]{0:T(1024)} %param.20) | copy-start | bytes 24580
  77.2 13.0 %copy-start.3 = (bf16[2048]{0:T(1024)(128)(2,1)S(1)}, bf16[2048]{0:T(1024)(128)(2,1)}, u32[]{:S(2)}) copy-start(bf16[2048]{0:T(1024)(128)(2,1)} %param.29) | copy-start | bytes 12292
  77.2 13.0 %copy-start.5 = (s32[1,64,4]{1,2,0:T(4,128)S(1)}, s32[1,64,4]{1,2,0:T(4,128)}, u32[]{:S(2)}) copy-start(s32[1,64,4]{1,2,0:T(4,128)} %param.21) | copy-start | bytes 3076
  77.2 13.0 %copy-start.6 = (f32[1,64,4]{1,2,0:T(4,128)S(1)}, f32[1,64,4]{1,2,0:T(4,128)}, u32[]{:S(2)}) copy-start(f32[1,64,4]{1,2,0:T(4,128)} %param.22) | copy-start | bytes 3076
  90.2 166.1 %reduce-scatter.2.cloned.1.call-start = ((), (), s32[]{:S(2)}) async-start(), calls=%async_computation.7 | async-start | bytes 4456448 | tf_op jit(solution)/shard_map/reduce_scatter | solution.py:108
  161.0 7.7 %copy-start.7 = (bf16[2048,704]{0,1:T(8,128)(2,1)S(1)}, bf16[2048,704]{0,1:T(8,128)(2,1)}, u32[]{:S(2)}) copy-start(bf16[2048,704]{0,1:T(8,128)(2,1)} %param.26) | copy-start | bytes 8650756
Sparse Core Ops, SparseCore 0:
  45.5 29.0 all-gather.3
  90.3 50.2 all-gather.5
  185.1 71.0 reduce-scatter.1

commit v2 on v1

--- a/solution.py
+++ b/solution.py
@@ -1,8 +1,11 @@
+import functools
 import math
 
 import jax
 import jax.numpy as jnp
 from jax import lax
+from jax.experimental import pallas as pl
+from jax.experimental.pallas import tpu as pltpu
 from jax.sharding import PartitionSpec as P
 
 HD = 128
@@ -59,15 +62,443 @@
     return jnp.dot(hidden, down_matrix, preferred_element_type=jnp.float32)
 
 
-def gathered_layer(residual, normed, expert_ids, gate_vals, gate, up, down, shared, score):
-    everyone = ("seq", "dp")
+MESH = pl.DeviceIdType.MESH
+
+
+def remote(src, dst, send_sem, recv_sem, **where):
+    return pltpu.make_async_remote_copy(
+        src_ref=src,
+        dst_ref=dst,
+        send_sem=send_sem,
+        recv_sem=recv_sem,
+        device_id=where,
+        device_id_type=MESH,
+    )
+
+
+def greet(peers):
+    barrier = pltpu.get_barrier_semaphore()
+
+    def hello(where):
+        pl.semaphore_signal(barrier, inc=1, device_id=where, device_id_type=MESH)
+
+    for ok, where in peers:
+        if ok is True:
+            hello(where)
+        else:
+            pl.when(ok)(functools.partial(hello, where))
+
+    always = sum(1 for ok, _ in peers if ok is True)
+    some = [ok for ok, _ in peers if ok is not True]
+    if not some:
+        pl.semaphore_wait(barrier, always)
+        return
+    first, second = some
+
+    @pl.when(first & second)
+    def _():
+        pl.semaphore_wait(barrier, always + 2)
+
+    @pl.when(first != second)
+    def _():
+        pl.semaphore_wait(barrier, always + 1)
+
+
+def neighbours(s, d, batch):
+    return [
+        (True, {"seq": flip(s, 1), "dp": d}),
+        (True, {"seq": flip(s, 2), "dp": d}),
+        (d > 0, {"seq": s, "dp": d - 1}),
+        (d < batch - 1, {"seq": s, "dp": d + 1}),
+    ]
+
+
+def flip(s, bit):
+    return s + bit - 2 * bit * ((s // bit) % 2)
+
+
+def line_kernel(seqs, batch, x_ref, t_ref, o_ref, ot_ref, zs, zr, ts, tr, ls):
+    s, d = lax.axis_index("seq"), lax.axis_index("dp")
+    n = seqs * batch
+    me = s * batch + d
+    others = []
+    for k in range(1, n):
+        to = lax.rem(me + k, n)
+        others.append((True, {"seq": to // batch, "dp": lax.rem(to, batch)}))
+    greet(others)
+    own = pltpu.make_async_copy(x_ref, o_ref.at[d], ls.at[0])
+    own_t = pltpu.make_async_copy(t_ref, ot_ref.at[me], ls.at[1])
+    own.start()
+    own_t.start()
+
+    def step(way, k, block, src):
+        return remote(
+            src, o_ref.at[block], zs.at[way, k], zr.at[way, k], seq=s, dp=d + 1 - 2 * way
+        )
+
+    def sends(way, k):
+        held = d >= k if way == 0 else d + k < batch
+        return held & (d < batch - 1 if way == 0 else d > 0)
+
+    def gets(way, k):
+        return d - 1 - k >= 0 if way == 0 else d + 1 + k < batch
+
+    for k in range(batch):
+        for way in range(2):
+            if k > 0:
+
+                @pl.when(gets(way, k - 1))
+                def _():
+                    step(way, k - 1, d, x_ref).wait_recv()
+
+            if k < batch - 1:
+
+                @pl.when(sends(way, k))
+                def _():
+                    block = d - k + 2 * k * way
+                    step(way, k, block, x_ref if k == 0 else o_ref.at[block]).start()
+
+        if k == 0:
+            for j, (_, where) in enumerate(others):
+                remote(t_ref, ot_ref.at[me], ts.at[j], tr.at[j], **where).start()
+    for k in range(batch - 1):
+        for way in range(2):
+
+            @pl.when(sends(way, k))
+            def _():
+                step(way, k, d, x_ref).wait_send()
+
+    for j, (_, where) in enumerate(others):
+        copy = remote(t_ref, ot_ref.at[me], ts.at[j], tr.at[j], **where)
+        copy.wait_send()
+        copy.wait_recv()
+    own.wait()
+    own_t.wait()
+
+
+def pool_kernel(seqs, batch, x_ref, o_ref, ws, wr, bs, br, ys, yr, ps, pr, hs, hr, ls):
+    s, d = lax.axis_index("seq"), lax.axis_index("dp")
+    far, near = flip(s, 2), flip(s, 1)
+    half = x_ref.shape[0] // 2
+    low, high = pl.ds(0, half), pl.ds(half, half)
+    greet(neighbours(s, d, batch))
+
+    def at(ss, dd):
+        return o_ref.at[ss * batch + dd]
+
+    def wide(way, k, block, src):
+        return remote(src, at(s, block), ws.at[way, k], wr.at[way, k], seq=s, dp=d + 1 - 2 * way)
+
+    def thin(way, k, block):
+        part = at(far, block).at[high]
+        return remote(part, part, bs.at[way, k], br.at[way, k], seq=s, dp=d + 1 - 2 * way)
+
+    def across(block):
+        part = at(s, block).at[low]
+        return remote(part, part, ys.at[block], yr.at[block], seq=far, dp=d)
+
+    def across_own():
+        return remote(x_ref, at(s, d), ys.at[batch], yr.at[batch], seq=far, dp=d)
+
+    def beside(block, src=None):
+        to = at(s, block)
+        return remote(to if src is None else src, to, ps.at[block], pr.at[block], seq=near, dp=d)
+
+    def beside_far(block, top):
+        part = at(far, block).at[high if top else low]
+        return remote(part, part, hs.at[top, block], hr.at[top, block], seq=near, dp=d)
+
+    def sends(way, k):
+        held = d >= k if way == 0 else d + k < batch
+        return held & (d < batch - 1 if way == 0 else d > 0)
+
+    def gets(way, k):
+        return d - 1 - k >= 0 if way == 0 else d + 1 + k < batch
+
+    own = pltpu.make_async_copy(x_ref, at(s, d), ls.at[0])
+    own.start()
+    for way in range(2):
+
+        @pl.when(sends(way, 0))
+        def _():
+            wide(way, 0, d, x_ref).start()
+
+    across_own().start()
+    beside(d, x_ref).start()
+    for k in range(1, batch + 1):
+        for way in range(2):
+            sign = 2 * way - 1
+            if k < batch:
+
+                @pl.when(gets(way, k - 1))
+                def _():
+                    wide(way, k - 1, d, x_ref).wait_recv()
+
+                if k < batch - 1:
+
+                    @pl.when(sends(way, k))
+                    def _():
+                        wide(way, k, d + sign * k, at(s, d + sign * k)).start()
+
+                @pl.when(gets(way, k - 1))
+                def _():
+                    across(d + sign * k).start()
+                    beside(d + sign * k).start()
+
+            if k > 1:
+
+                @pl.when(gets(way, k - 2))
+                def _():
+                    thin(way, k - 2, d).wait_recv()
+
+                if k < batch:
+
+                    @pl.when(sends(way, k - 1))
+                    def _():
+                        thin(way, k - 1, d + sign * (k - 1)).start()
+
+                @pl.when(gets(way, k - 2))
+                def _():
+                    beside_far(d + sign * (k - 1), 1).start()
+
+        if k == 1:
+            across_own().wait_recv()
+            for way in range(2):
+
+                @pl.when(sends(way, 0))
+                def _():
+                    thin(way, 0, d).start()
+
+            beside_far(d, 0).start()
+            beside_far(d, 1).start()
+    for off in range(1, batch):
+        block = lax.rem(d + off, batch)
+        across(block).wait_recv()
+        beside_far(block, 0).start()
+    for block in range(batch):
+        beside(block).wait_recv()
+        beside_far(block, 0).wait_recv()
+        beside_far(block, 1).wait_recv()
+    for k in range(batch - 1):
+        for way in range(2):
+
+            @pl.when(sends(way, k))
+            def _():
+                wide(way, k, d, x_ref).wait_send()
+                thin(way, k, d).wait_send()
+
+    across_own().wait_send()
+    for off in range(1, batch):
+        across(lax.rem(d + off, batch)).wait_send()
+    for block in range(batch):
+        beside(block).wait_send()
+        beside_far(block, 0).wait_send()
+        beside_far(block, 1).wait_send()
+    own.wait()
+
+
+def scatter_kernel(
+    seqs, batch, x_ref, o_ref, near_buf, acc, y_buf, yb_buf, z_buf, ds, dr, ys, yr, zs, zr
+):
+    s, d = lax.axis_index("seq"), lax.axis_index("dp")
+    far, near, cross = flip(s, 2), flip(s, 1), flip(flip(s, 1), 2)
+    half = x_ref.shape[1] // 2
+    low, high = pl.ds(0, half), pl.ds(half, half)
+    greet(neighbours(s, d, batch))
+
+    def chip(which, block):
+        row = (cross if which else near) * batch + block
+        return remote(
+            x_ref.at[row],
+            near_buf.at[which, block],
+            ds.at[which, block],
+            dr.at[which, block],
+            seq=near,
+            dp=d,
+        )
+
+    def add(a, b):
+        return (a.astype(jnp.float32) + b.astype(jnp.float32)).astype(jnp.bfloat16)
+
+    def across(block):
+        return remote(
+            acc.at[1, block, low], y_buf.at[block], ys.at[block], yr.at[block], seq=far, dp=d
+        )
+
+    def across_last():
+        return remote(
+            acc.at[1, d, high], yb_buf, ys.at[batch], yr.at[batch], seq=far, dp=d
+        )
+
+    flows = ((1, high), (0, high), (0, low))
+
+    def hop(flow, way, block):
+        which, part = flows[flow]
+        return remote(
+            acc.at[which, block, part],
+            z_buf.at[flow, way, block],
+            zs.at[flow, block],
+            zr.at[flow, way, block],
+            seq=s,
+            dp=d + 1 - 2 * way,
+        )
+
+    def merge(flow, way, block):
+        which, part = flows[flow]
+        hop(flow, way, block).wait_recv()
+        acc[which, block, part] = add(acc[which, block, part], z_buf[flow, way, block])
+
+    for which in (1, 0):
+        for block in range(batch):
+            chip(which, block).start()
+    for which in (1, 0):
+        for block in range(batch):
+            chip(which, block).wait_recv()
+            row = (far if which else s) * batch + block
+            acc[which, block] = add(x_ref[row], near_buf[which, block])
+            if which:
+                across(block).start()
+
+    def line(flow):
+        for k in range(batch - 1):
+            for way in range(2):
+                block = k if way else batch - 1 - k
+                inner = d < batch - 1 if way else d > 0
+
+                @pl.when((d > block if way else d < block) & inner)
+                def _():
+                    merge(flow, way, block)
+
+                @pl.when(d > block if way else d < block)
+                def _():
+                    hop(flow, way, block).start()
+
+    def land(flow):
+        for way in range(2):
+
+            @pl.when(d < batch - 1 if way else d > 0)
+            def _():
+                merge(flow, way, d)
+
+    line(0)
+    line(1)
+    for block in range(batch):
+        across(block).wait_recv()
+        acc[0, block, low] = add(acc[0, block, low], y_buf[block])
+    line(2)
+    land(0)
+    across_last().start()
+    land(1)
+    land(2)
+    across_last().wait_recv()
+    acc[0, d, high] = add(acc[0, d, high], yb_buf[...])
+    o_ref[...] = acc[0, d]
+    for which in (1, 0):
+        for block in range(batch):
+            chip(which, block).wait_send()
+    for block in range(batch):
+        across(block).wait_send()
+    across_last().wait_send()
+    for flow in range(3):
+        for block in range(batch):
+
+            @pl.when(d < block)
+            def _():
+                hop(flow, 0, block).wait_send()
+
+            @pl.when(d > block)
+            def _():
+                hop(flow, 1, block).wait_send()
+
+
+VMEM = pl.BlockSpec(memory_space=pltpu.VMEM)
+DMA = pltpu.SemaphoreType.DMA
+
+
+def params(number):
+    return pltpu.CompilerParams(
+        collective_id=number, has_side_effects=True, vmem_limit_bytes=24 << 20
+    )
+
+
+def line_gather(x, table):
+    seqs, batch = lax.axis_size("seq"), lax.axis_size("dp")
+    n = seqs * batch
+    return pl.pallas_call(
+        functools.partial(line_kernel, seqs, batch),
+        out_shape=(
+            jax.ShapeDtypeStruct((batch,) + x.shape, x.dtype),
+            jax.ShapeDtypeStruct((n,) + table.shape, table.dtype),
+        ),
+        in_specs=[VMEM, VMEM],
+        out_specs=(VMEM, VMEM),
+        scratch_shapes=[
+            DMA((2, batch)),
+            DMA((2, batch)),
+            DMA((n,)),
+            DMA((n,)),
+            DMA((2,)),
+        ],
+        compiler_params=params(1),
+    )(x, table)
+
+
+def pool_gather(x):
+    seqs, batch = lax.axis_size("seq"), lax.axis_size("dp")
+    return pl.pallas_call(
+        functools.partial(pool_kernel, seqs, batch),
+        out_shape=jax.ShapeDtypeStruct((seqs * batch,) + x.shape, x.dtype),
+        in_specs=[VMEM],
+        out_specs=VMEM,
+        scratch_shapes=[
+            DMA((2, batch)),
+            DMA((2, batch)),
+            DMA((2, batch)),
+            DMA((2, batch)),
+            DMA((batch + 1,)),
+            DMA((batch + 1,)),
+            DMA((batch,)),
+            DMA((batch,)),
+            DMA((2, batch)),
+            DMA((2, batch)),
+            DMA((1,)),
+        ],
+        compiler_params=params(2),
+    )(x)
+
+
+def pool_scatter(x):
+    seqs, batch = lax.axis_size("seq"), lax.axis_size("dp")
+    tokens, width = x.shape[1:]
+    half = tokens // 2
+    return pl.pallas_call(
+        functools.partial(scatter_kernel, seqs, batch),
+        out_shape=jax.ShapeDtypeStruct((tokens, width), x.dtype),
+        in_specs=[VMEM],
+        out_specs=VMEM,
+        scratch_shapes=[
+            pltpu.VMEM((2, batch, tokens, width), x.dtype),
+            pltpu.VMEM((2, batch, tokens, width), x.dtype),
+            pltpu.VMEM((batch, half, width), x.dtype),
+            pltpu.VMEM((half, width), x.dtype),
+            pltpu.VMEM((3, 2, batch, half, width), x.dtype),
+            DMA((2, batch)),
+            DMA((2, batch)),
+            DMA((batch + 1,)),
+            DMA((batch + 1,)),
+            DMA((3, batch)),
+            DMA((3, 2, batch)),
+        ],
+        compiler_params=params(3),
+    )(x)
+
+
+def gathered_layer(residual, normed, table, gate, up, down, shared, score):
     seq_count, batch_count = lax.axis_size("seq"), lax.axis_size("dp")
     devices = seq_count * batch_count
     tokens, width = normed.shape
     own_experts = gate.shape[0] // SPLIT
     room = devices * CAP
-    table = jnp.concatenate([expert_ids[0].astype(jnp.float32), gate_vals[0]], axis=1)
-    table = lax.all_gather(table, everyone, axis=0, tiled=True)
     me = lax.axis_index("seq") * batch_count + lax.axis_index("dp")
     mine = (me * own_experts + jnp.arange(own_experts)).astype(jnp.float32)
     named = (table[:, :TOPK, None] == mine).astype(jnp.float32)
@@ -82,7 +513,7 @@
     slot_gate = jnp.sum(jnp.where(pick, weight.T[:, None, :], 0.0), axis=-1)
     pick = pick.astype(jnp.bfloat16).reshape(own_experts * room, total)
 
-    pool = lax.all_gather(normed, everyone, axis=0, tiled=True)
+    pool = pool_gather(normed).reshape(total, width)
     rows = jnp.dot(pick, pool, preferred_element_type=jnp.float32).astype(jnp.bfloat16)
     rows = rows.reshape(own_experts, room, width)
     gate = gate.reshape((own_experts, SPLIT) + gate.shape[1:])
@@ -105,9 +536,7 @@
     shared_part = shared_block(line, *shared) * share_weight[:, None]
     here = (jnp.arange(seq_count) == s)[:, None, None]
     partial = jnp.where(here, partial + shared_part[None], partial).astype(jnp.bfloat16)
-    summed = lax.psum_scatter(
-        partial.reshape(total, width), everyone, scatter_dimension=0, tiled=True
-    )
+    summed = pool_scatter(partial.reshape(devices, tokens, width))
     out = residual.astype(jnp.float32) + summed.astype(jnp.float32)
     return out.astype(jnp.bfloat16)[None]
 
@@ -146,8 +575,17 @@
     own_attended = lax.all_to_all(
         by_position, "seq", split_axis=0, concat_axis=2, tiled=True
     ).reshape(tokens, model_width)
+    dense = expert_gate.shape[0] % SPLIT == 0 and seq_count == 4 and batch_count > 1 and tokens % 32 == 0
+    if dense:
+        table = jnp.concatenate([expert_ids[0].astype(jnp.float32), gate_vals[0]], axis=1)
+        table = jnp.pad(table.T, ((0, 0), (0, -tokens % 128)))
+        gathered, table = line_gather(own_attended, table)
+        gathered = gathered.reshape(batch_count * tokens, model_width)
+        table = table[:, :, :tokens].swapaxes(1, 2).reshape(-1, 2 * TOPK)
+    else:
+        gathered = lax.all_gather(own_attended, "dp", axis=0, tiled=True)
     column_block = jnp.dot(
-        lax.all_gather(own_attended, "dp", axis=0, tiled=True),
+        gathered,
         out_weight,
         preferred_element_type=jnp.float32,
     ).astype(jnp.bfloat16)
@@ -157,12 +595,11 @@
     normed = (
         stream * lax.rsqrt(jnp.mean(stream * stream, axis=-1, keepdims=True) + norm_eps) * norm_gain
     ).astype(jnp.bfloat16)
-    if expert_gate.shape[0] % SPLIT == 0:
+    if dense:
         return gathered_layer(
             residual,
             normed,
-            expert_ids,
-            gate_vals,
+            table,
             expert_gate,
             expert_up,
             expert_down,

time: 265 us -> 194 us (0.73)
  waiting for transfers between devices: 130 us -> 21.6 us
  Pallas kernels: 0 us -> 99.5 us
  blocking collectives: 51.1 us -> 0 us
  between operations: 13.4 us -> 0.33 us
  starting transfers between devices: 7.86 us -> 14.9 us
  matrix products: 51.4 us -> 45.2 us
    pallas_call x0 -> x3, Pallas kernels: none -> 99.5 us  [the longest x1 43 us: pool_scatter(): pl.pallas_call(functools.partial(scatter_kernel, seqs, batch), out_shape=...]
    reduce_scatter x1 -> x0, waiting for transfers between devices: 71.3 us -> none  [gathered_layer(): lax.psum_scatter(partial.reshape(total, width), everyone, scatter_dimensi...]
    all_gather x2 -> x0, waiting for transfers between devices: 47.2 us -> none  [the longest x1 29.2 us: body(): lax.all_gather(own_attended, 'dp', axis=0, tiled=True)]
    all_gather x1 -> x0, blocking collectives: 31 us -> none  [gathered_layer(): table = lax.all_gather(table, everyone, axis=0, tiled=True)]
    all_to_all x2 -> x0, blocking collectives: 20.1 us -> none  [the longest x1 11.7 us: body(): lax.all_to_all(column_block, 'dp', split_axis=0, concat_axis=1, tiled=True)]
    all_to_all x0 -> x2, waiting for transfers between devices: none -> 10.6 us  [the longest x1 5.94 us: body(): lax.all_to_all(by_position, 'seq', split_axis=0, concat_axis=2, tiled=True)]
    all_to_all x0 -> x2, starting transfers between devices: none -> 7.11 us  [the longest x1 3.71 us: body(): lax.all_to_all(column_block, 'dp', split_axis=0, concat_axis=1, tiled=True)]
  transfers between devices with their start and end apart: 5 -> 4, of which waited for: 5 -> 4; matrix products, arithmetic and copies ran while one was open for 2% -> 3% of each run, Pallas kernels for 0% -> 0%
where the time goes in v2:
time: 194 us; the launch traced here: 193 us
  Pallas kernels  99.5 us (51%)
  matrix products  45.2 us (23%)
  waiting for transfers between devices  21.6 us (11%)
  starting transfers between devices  14.9 us (8%)
  local copies, waits for them, and re-layouts  7.68 us (4%)
  other arithmetic  3.92 us (2%)
    pallas_call x1, Pallas kernels, pool_scatter(): pl.pallas_call(functools.partial(scatter_kernel, seqs, batch), out_shape=...  43 us
    pallas_call x1, Pallas kernels, pool_gather(): pl.pallas_call(functools.partial(pool_kernel, seqs, batch), out_shape=jax...  31.3 us
    pallas_call x1, Pallas kernels, line_gather(): pl.pallas_call(functools.partial(line_kernel, seqs, batch), out_shape=(ja...  25.2 us
    dot_general x1, matrix products, gathered_layer(): jnp.einsum('ecd,ebdf->ebcf', rows, up, preferred_element_type=jnp.float32)  8.64 us
    dot_general x1, matrix products, gathered_layer(): jnp.einsum('ebcf,ebfd->ecd', hidden, down, preferred_element_type=jnp.flo...  7.56 us
    dot_general x1, matrix products, shared_block(): return jnp.dot(hidden, down_matrix, preferred_element_type=jnp.float32)  7.13 us
    all_to_all x1, waiting for transfers between devices, body(): lax.all_to_all(paired, 'seq', split_axis=2, concat_axis=1, tiled=True)  6.8 us
    all_to_all x1, waiting for transfers between devices, body(): lax.all_to_all(by_position, 'seq', split_axis=0, concat_axis=2, tiled=True)  5.94 us
  transfers between devices with their start and end apart: 4, of which 4 were waited for; matrix products, arithmetic and copies ran while one was open for 3% of the time, Pallas kernels for 0%

profile of v2, /device:TPU:0, one launch (start us, length us, event | category | flops | bytes accessed | tf_op | source)
XLA Modules:
  0.0 193.1 jit_solution(1074323535567029194)
XLA Ops:
  0.0 0.0 copy-start
  0.0 0.0 copy-start.6
  0.0 0.0 copy-start.7
  0.0 0.0 copy-start.5
  0.0 1.3 reshape.159
  1.3 0.8 copy.57
  2.1 4.3 %all-to-all-start.1 = ((bf16[1,64,4,4,128]{4,1,3,0,2:T(8,128)(2,1)}), bf16[1,64,4,4,128]{4,1,3,0,2:T(8,128)(2,1)}, u32[]{:S(2)}, u32[]{:S(2)}) async-start(bf16[1,64,4,4,128]{4,1,3,0,2:T(8,128)(2,1)} %copy.57), calls=%async_computation.1 | async-start | bytes 524288 | tf_op jit(solution)/shard_map/all_to_all | solution.py:570
  6.3 1.4 reshape.158
  7.7 0.9 copy.54
  8.7 4.2 %all-to-all-done.1 = bf16[1,64,4,4,128]{4,1,3,0,2:T(8,128)(2,1)} async-done(((bf16[1,64,4,4,128]{4,1,3,0,2:T(8,128)(2,1)}), bf16[1,64,4,4,128]{4,1,3,0,2:T(8,128)(2,1)}, u32[]{:S(2)}, u32[]{:S(2)}) %all-to-all-start.1) | async-done | bytes 262176 | tf_op jit(solution)/shard_map/all_to_all | solution.py:570
  12.9 3.5 %all-to-all-start = ((bf16[2,64,4,4,128]{4,1,3,0,2:T(8,128)(2,1)}), bf16[2,64,4,4,128]{4,1,3,0,2:T(8,128)(2,1)S(1)}, u32[]{:S(2)}, u32[]{:S(2)}) async-start(bf16[2,64,4,4,128]{4,1,3,0,2:T(8,128)(2,1)} %copy.54), calls=%async_computation | async-start | bytes 1048576 | tf_op jit(solution)/shard_map/all_to_all | solution.py:569
  16.4 0.0 copy-done.6
  16.4 0.0 copy-done.4
  16.4 0.1 eq.87
  16.5 0.0 copy-done.7
  16.5 0.0 copy-done.5
  16.6 0.1 fusion.36
  16.7 1.7 copy.58
  18.3 6.8 %all-to-all-done = bf16[2,64,4,4,128]{4,1,3,0,2:T(8,128)(2,1)S(1)} async-done(((bf16[2,64,4,4,128]{4,1,3,0,2:T(8,128)(2,1)}), bf16[2,64,4,4,128]{4,1,3,0,2:T(8,128)(2,1)S(1)}, u32[]{:S(2)}, u32[]{:S(2)}) %all-to-all-start) | async-done | bytes 524320 | tf_op jit(solution)/shard_map/all_to_all | solution.py:569
  25.2 0.5 fusion.51
  25.7 1.3 fusion.11
  27.0 2.1 %fusion.15 = bf16[256,4,128]{2,0,1:T(8,128)(2,1)S(1)} fusion(bf16[256,4,128]{2,0,1:T(8,128)(2,1)} %bitcast.133, f32[4,256]{1,0:T(4,128)S(1)} %fusion.51, f32[4,256,256]{1,2,0:T(8,128)} %fusion.11), kind=kOutput, calls=%fused_computation.30 | convolution fusion | flops 68027648 | bytes 1576960 | tf_op jit(solution)/shard_map/hqk,khd->qhd/dot_general | solution.py:42
  29.1 0.2 copy.60
  29.4 0.8 reshape.160
  30.2 3.4 %all-to-all-start.2 = ((bf16[4,64,512]{2,1,0:T(8,128)(2,1)}), bf16[4,64,512]{2,1,0:T(8,128)(2,1)S(1)}, u32[]{:S(2)}, u32[]{:S(2)}) async-start(bf16[4,64,512]{2,1,0:T(8,128)(2,1)} %reshape.160), calls=%async_computation.2 | async-start | bytes 524288 | tf_op jit(solution)/shard_map/all_to_all | solution.py:575
  33.6 5.9 %all-to-all-done.2 = bf16[4,64,512]{2,1,0:T(8,128)(2,1)S(1)} async-done(((bf16[4,64,512]{2,1,0:T(8,128)(2,1)}), bf16[4,64,512]{2,1,0:T(8,128)(2,1)S(1)}, u32[]{:S(2)}, u32[]{:S(2)}) %all-to-all-start.2) | async-done | bytes 262176 | tf_op jit(solution)/shard_map/all_to_all | solution.py:575
  39.5 0.2 copy.61
  39.8 25.2 %shard_map.145 = (bf16[4,64,2048]{2,1,0:T(8,128)(2,1)S(1)}, f32[16,8,128]{2,1,0:T(8,128)S(1)}) custom-call(bf16[64,2048]{1,0:T(8,128)(2,1)S(1)} %bitcast.116, f32[8,128]{1,0:T(8,128)S(1)} %pad.4.t_ref), custom_call_target="tpu_custom_call" | custom-call | tf_op jit(solution)/shard_map/pallas_call | solution.py:427
  65.0 3.0 %convolution_convert_fusion.1 = bf16[256,512]{1,0:T(8,128)(2,1)} fusion(bf16[256,2048]{1,0:T(8,128)(2,1)S(1)} %bitcast.117, bf16[2048,512]{1,0:T(8,128)(2,1)} %param.19), kind=kOutput, calls=%fused_computation.28 | convolution fusion | flops 537001984 | bytes 3407872 | tf_op jit(solution)/shard_map/dot_general | solution.py:587
  68.0 3.7 %all-to-all-start.3 = ((bf16[4,64,512]{2,1,0:T(8,128)(2,1)}), bf16[4,64,512]{2,1,0:T(8,128)(2,1)S(1)}, u32[]{:S(2)}, u32[]{:S(2)}) async-start(bf16[4,64,512]{2,1,0:T(8,128)(2,1)} %bitcast.17), calls=%async_computation.3 | async-start | bytes 524288 | tf_op jit(solution)/shard_map/all_to_all | solution.py:592
  71.7 0.0 copy-start.3
  71.7 0.1 reshape.163
  71.8 0.1 fusion.38
  71.9 0.5 fusion.16
  72.4 0.3 bitcast_compare_fusion
  72.7 0.2 select_reduce_fusion
  72.9 0.9 iota_compare_fusion.2
  73.8 4.7 %all-to-all-done.3 = bf16[4,64,512]{2,1,0:T(8,128)(2,1)S(1)} async-done(((bf16[4,64,512]{2,1,0:T(8,128)(2,1)}), bf16[4,64,512]{2,1,0:T(8,128)(2,1)S(1)}, u32[]{:S(2)}, u32[]{:S(2)}) %all-to-all-start.3) | async-done | bytes 262176 | tf_op jit(solution)/shard_map/all_to_all | solution.py:592
  78.5 0.0 slice-start
  78.6 1.3 fusion.29
  79.9 0.0 copy-done.3
  79.9 0.0 copy-start.8
  79.9 0.1 fusion.31.x_ref
  80.0 0.0 slice-start.1
  80.0 31.3 %shard_map.146 = bf16[16,64,2048]{2,1,0:T(8,128)(2,1)S(1)} custom-call(bf16[64,2048]{1,0:T(8,128)(2,1)S(1)} %fusion.31.x_ref), custom_call_target="tpu_custom_call" | custom-call | tf_op jit(solution)/shard_map/pallas_call | solution.py:448
  111.3 0.0 copy-start.1
  111.3 0.4 fusion.17
  111.7 0.0 copy-start.2
  111.7 0.0 copy-done.8
  111.7 1.9 fusion.20
  113.7 0.0 copy-done.1
  113.7 0.0 copy-done.2
  113.7 2.6 %convolution_convert_fusion = bf16[320,2048]{1,0:T(8,128)(2,1)} fusion(pred[320,1024]{1,0:T(32,128)(4,1)S(1)} %bitcast.132, bf16[1024,2048]{1,0:T(8,128)(2,1)S(1)} %bitcast.113), kind=kOutput, calls=%fused_computation.9 | convolution fusion | flops 1342832640 | bytes 5832704 | tf_op jit(solution)/shard_map/dot_general | solution.py:517
  116.3 0.0 slice-done
  116.3 0.0 slice-done.1
  116.3 0.0 slice-done.2
  116.3 5.2 %fusion.52 = f32[2,160,4,352]{3,1,2,0:T(8,128)S(1)} fusion(bf16[2,160,2048,1]{2,1,3,0:T(8,128)(2,1)} %bitcast.123, bf16[2,4,2048,352]{2,3,1,0:T(8,128)(2,1)S(1)} %bitcast.120), kind=kOutput, calls=%fused_computation.79 | convolution fusion | flops 1845493760 | bytes 14647296 | tf_op jit(solution)/shard_map/ecd,ebdf->ebcf/dot_general | solution.py:522
  121.5 8.6 %fusion.5 = bf16[2,4,160,352]{3,2,1,0:T(8,128)(2,1)S(1)} fusion(f32[2,160,4,352]{3,1,2,0:T(8,128)S(1)} %fusion.52, bf16[2,160,2048,1]{2,1,3,0:T(8,128)(2,1)} %bitcast.124, bf16[2,4,2048,352]{2,3,1,0:T(8,128)(2,1)} %bitcast.138), kind=kOutput, calls=%fused_computation.11 | convolution fusion | flops 1848197120 | bytes 15548416 | tf_op jit(solution)/shard_map/ecd,ebdf->ebcf/dot_general | solution.py:523
  130.1 7.6 %fusion.4 = bf16[2,160,2048]{2,1,0:T(8,128)(2,1)} fusion(bf16[2,4,160,352]{3,2,1,0:T(8,128)(2,1)S(1)} %fusion.5, bf16[2,4,352,2048]{3,2,1,0:T(8,128)(2,1)} %bitcast.139, f32[2,160]{1,0:T(2,128)S(1)} %select_reduce_fusion), kind=kOutput, calls=%fused_computation.8 | convolution fusion | flops 1846804480 | bytes 13747456 | tf_op jit(solution)/shard_map/ebcf,ebfd->ecd/dot_general | solution.py:525
  137.7 0.0 copy-done
  137.7 7.1 %convolution_multiply_fusion = f32[256,2048]{1,0:T(8,128)} fusion(bf16[704,2048]{1,0:T(8,128)(2,1)S(1)} %copy-done, f32[256]{0:T(256)S(1)} %add_divide_fusion, bf16[2048,704]{0,1:T(8,128)(2,1)} %param.27, bf16[1024,2048]{1,0:T(8,128)(2,1)} %bitcast.114, s32[]{:T(128)S(6)} %select_n.23, f32[256,704]{0,1:T(8,128)} %fusion.20), kind=kOutput, calls=%fused_computation.7 | convolution fusion | flops 1478000640 | bytes 9634820 | tf_op jit(solution)/shard_map/dot_general | solution.py:62
  144.8 4.4 %fusion.1 = bf16[4,256,2048]{2,1,0:T(8,128)(2,1)S(1)} fusion(f32[256,2048]{1,0:T(8,128)} %convolution_multiply_fusion, pred[4]{0:T(512)(128)(4,1)S(1)} %iota_compare_fusion.6, bf16[320,2048,1]{1,0,2:T(8,128)(2,1)} %bitcast.140, pred[40,4,8,256]{3,2,1,0:T(8,128)(4,1)S(1)} %bitcast.131), kind=kOutput, calls=%fused_computation.2 | convolution fusion | flops 1348468736 | bytes 7929860 | tf_op jit(solution)/shard_map/dot_general | solution.py:527
  149.2 43.0 %shard_map.147 = bf16[64,2048]{1,0:T(8,128)(2,1)S(1)} custom-call(bf16[16,64,2048]{2,1,0:T(8,128)(2,1)S(1)} %bitcast.115), custom_call_target="tpu_custom_call" | custom-call | tf_op jit(solution)/shard_map/pallas_call | solution.py:474
  192.3 0.8 fusion.35
  (21 shorter events, 0.3 us)
Async XLA Ops:
  0.0 137.7 %copy-start = (bf16[704,2048]{1,0:T(8,128)(2,1)S(1)}, bf16[704,2048]{1,0:T(8,128)(2,1)}, u32[]{:S(2)}) copy-start(bf16[704,2048]{1,0:T(8,128)(2,1)} %param.28) | copy-start | bytes 8650756
  0.0 16.4 %copy-start.6 = (s32[1,64,4]{1,2,0:T(4,128)S(1)}, s32[1,64,4]{1,2,0:T(4,128)}, u32[]{:S(2)}) copy-start(s32[1,64,4]{1,2,0:T(4,128)} %param.21) | copy-start | bytes 3076
  0.0 16.4 %copy-start.4 = (bf16[2048]{0:T(1024)(128)(2,1)S(1)}, bf16[2048]{0:T(1024)(128)(2,1)}, u32[]{:S(2)}) copy-start(bf16[2048]{0:T(1024)(128)(2,1)} %param.29) | copy-start | bytes 12292
  0.0 16.5 %copy-start.7 = (f32[1,64,4]{1,2,0:T(4,128)S(1)}, f32[1,64,4]{1,2,0:T(4,128)}, u32[]{:S(2)}) copy-start(f32[1,64,4]{1,2,0:T(4,128)} %param.22) | copy-start | bytes 3076
  0.0 16.5 %copy-start.5 = (s32[1,256]{1,0:T(1,128)S(1)}, s32[1,256]{1,0:T(1,128)}, u32[]{:S(2)}) copy-start(s32[1,256]{1,0:T(1,128)} %param.18) | copy-start | bytes 3076
  2.1 10.8 %all-to-all-start.1 = ((bf16[1,64,4,4,128]{4,1,3,0,2:T(8,128)(2,1)}), bf16[1,64,4,4,128]{4,1,3,0,2:T(8,128)(2,1)}, u32[]{:S(2)}, u32[]{:S(2)}) async-start(bf16[1,64,4,4,128]{4,1,3,0,2:T(8,128)(2,1)} %copy.57), calls=%async_computation.1 | async-start | bytes 524288 | tf_op jit(solution)/shard_map/all_to_all | solution.py:570
  12.9 12.3 %all-to-all-start = ((bf16[2,64,4,4,128]{4,1,3,0,2:T(8,128)(2,1)}), bf16[2,64,4,4,128]{4,1,3,0,2:T(8,128)(2,1)S(1)}, u32[]{:S(2)}, u32[]{:S(2)}) async-start(bf16[2,64,4,4,128]{4,1,3,0,2:T(8,128)(2,1)} %copy.54), calls=%async_computation | async-start | bytes 1048576 | tf_op jit(solution)/shard_map/all_to_all | solution.py:569
  30.2 9.4 %all-to-all-start.2 = ((bf16[4,64,512]{2,1,0:T(8,128)(2,1)}), bf16[4,64,512]{2,1,0:T(8,128)(2,1)S(1)}, u32[]{:S(2)}, u32[]{:S(2)}) async-start(bf16[4,64,512]{2,1,0:T(8,128)(2,1)} %reshape.160), calls=%async_computation.2 | async-start | bytes 524288 | tf_op jit(solution)/shard_map/all_to_all | solution.py:575
  68.0 10.5 %all-to-all-start.3 = ((bf16[4,64,512]{2,1,0:T(8,128)(2,1)}), bf16[4,64,512]{2,1,0:T(8,128)(2,1)S(1)}, u32[]{:S(2)}, u32[]{:S(2)}) async-start(bf16[4,64,512]{2,1,0:T(8,128)(2,1)} %bitcast.17), calls=%async_computation.3 | async-start | bytes 524288 | tf_op jit(solution)/shard_map/all_to_all | solution.py:592
  71.7 8.2 %copy-start.3 = (f32[2048]{0:T(1024)S(1)}, f32[2048]{0:T(1024)}, u32[]{:S(2)}) copy-start(f32[2048]{0:T(1024)} %param.20) | copy-start | bytes 24580
  78.5 37.8 %slice-start = ((s8[11534336]{0:T(1024)(128)(4,1)}), s8[4194304]{0:T(1024)(128)(4,1)S(1)}, s32[]{:S(2)}) async-start(s8[11534336]{0:T(1024)(128)(4,1)} %bitcast.118), calls=%async_computation.4 | async-start | bytes 8388608
  79.9 31.8 %copy-start.8 = (bf16[2048,704]{0,1:T(8,128)(2,1)S(1)}, bf16[2048,704]{0,1:T(8,128)(2,1)}, u32[]{:S(2)}) copy-start(bf16[2048,704]{0,1:T(8,128)(2,1)} %param.26) | copy-start | bytes 8650756
  80.0 36.2 %slice-start.1 = ((s8[11534336]{0:T(1024)(128)(4,1)}), s8[4194304]{0:T(1024)(128)(4,1)S(1)}, s32[]{:S(2)}) async-start(s8[11534336]{0:T(1024)(128)(4,1)} %bitcast.118), calls=%async_computation.5 | async-start | bytes 8388608
  111.3 2.4 %copy-start.1 = (bf16[16,64,2048]{2,1,0:T(8,128)(2,1)}, bf16[16,64,2048]{2,1,0:T(8,128)(2,1)S(1)}, u32[]{:S(2)}) copy-start(bf16[16,64,2048]{2,1,0:T(8,128)(2,1)S(1)} %shard_map.146) | copy-start | bytes 12582916
  111.7 2.0 %copy-start.2 = (pred[2,160,1024]{2,1,0:T(32,128)(4,1)S(1)}, pred[2,160,1024]{2,1,0:T(32,128)(4,1)}, u32[]{:S(2)}) copy-start(pred[2,160,1024]{2,1,0:T(32,128)(4,1)} %iota_compare_fusion.2) | copy-start | bytes 983044
  113.7 2.6 %slice-start.2 = ((s8[11534336]{0:T(1024)(128)(4,1)}), s8[3145728]{0:T(1024)(128)(4,1)S(1)}, s32[]{:S(2)}) async-start(s8[11534336]{0:T(1024)(128)(4,1)} %bitcast.118), calls=%async_computation.6 | async-start | bytes 6291456

commit v3 on v2

--- a/solution.py
+++ b/solution.py
@@ -117,19 +117,87 @@
     return s + bit - 2 * bit * ((s // bit) % 2)
 
 
-def line_kernel(seqs, batch, x_ref, t_ref, o_ref, ot_ref, zs, zr, ts, tr, ls):
+def line_kernel(
+    seqs, batch, q_ref, v_ref, row_ref, col_ref, t_ref, o_ref, ot_ref,
+    got, att, zs, zr, ts, tr, ls, qs, qr, ats, atr,
+):
     s, d = lax.axis_index("seq"), lax.axis_index("dp")
     n = seqs * batch
     me = s * batch + d
+    tokens, width = v_ref.shape
+    part = width // seqs
     others = []
     for k in range(1, n):
         to = lax.rem(me + k, n)
         others.append((True, {"seq": to // batch, "dp": lax.rem(to, batch)}))
     greet(others)
-    own = pltpu.make_async_copy(x_ref, o_ref.at[d], ls.at[0])
-    own_t = pltpu.make_async_copy(t_ref, ot_ref.at[me], ls.at[1])
+
+    def columns(who):
+        return pl.ds(pl.multiple_of(who * part, 128), part)
+
+    def rows(who):
+        return pl.ds(pl.multiple_of(who * tokens, 16), tokens)
+
+    def source(which):
+        return v_ref if which == 2 else q_ref.at[which]
+
+    def deal(which, k):
+        to = lax.rem(s + k, seqs)
+        return remote(
+            source(which).at[:, columns(to)],
+            got.at[which, rows(s)],
+            qs.at[which, k],
+            qr.at[which, k],
+            seq=to,
+            dp=d,
+        )
+
+    def keep(which):
+        return pltpu.make_async_copy(
+            source(which).at[:, columns(s)], got.at[which, rows(s)], ls.at[which]
+        )
+
+    def back(k):
+        to = lax.rem(s + k, seqs)
+        return remote(
+            att.at[rows(to)], o_ref.at[d, :, columns(s)], ats.at[k], atr.at[k], seq=to, dp=d
+        )
+
+    for which in range(3):
+        for k in range(1, seqs):
+            deal(which, k).start()
+        keep(which).start()
+    own_t = pltpu.make_async_copy(t_ref, ot_ref.at[me], ls.at[3])
+    own_t.start()
+    for which in range(3):
+        for k in range(1, seqs):
+            deal(which, k).wait_recv()
+        keep(which).wait()
+    length = tokens * seqs
+    seen = (
+        lax.broadcasted_iota(jnp.int32, (length, length), 0)
+        >= lax.broadcasted_iota(jnp.int32, (length, length), 1)
+    ) & (col_ref[...] == row_ref[...])
+    for h in range(part // HD):
+        at = pl.ds(h * HD, HD)
+        scores = lax.dot_general(
+            got[0, :, at], got[1, :, at], (((1,), (1,)), ((), ())),
+            preferred_element_type=jnp.float32,
+        )
+        scores = jnp.where(seen, scores * (1.0 / math.sqrt(HD)), -1e30)
+        lifted = jnp.exp(scores - jnp.max(scores, axis=-1, keepdims=True))
+        probs = (lifted / jnp.sum(lifted, axis=-1, keepdims=True)).astype(jnp.bfloat16)
+        att[:, at] = jnp.dot(
+            probs, got[2, :, at], preferred_element_type=jnp.float32
+        ).astype(jnp.bfloat16)
+    for k in range(1, seqs):
+        back(k).start()
+    own = pltpu.make_async_copy(att.at[rows(s)], o_ref.at[d, :, columns(s)], ls.at[4])
     own.start()
-    own_t.start()
+    for k in range(1, seqs):
+        back(k).wait_recv()
+    own.wait()
+    x_ref = o_ref.at[d]
 
     def step(way, k, block, src):
         return remote(
@@ -172,16 +240,51 @@
         copy = remote(t_ref, ot_ref.at[me], ts.at[j], tr.at[j], **where)
         copy.wait_send()
         copy.wait_recv()
-    own.wait()
     own_t.wait()
-
-
-def pool_kernel(seqs, batch, x_ref, o_ref, ws, wr, bs, br, ys, yr, ps, pr, hs, hr, ls):
+    for k in range(1, seqs):
+        back(k).wait_send()
+        for which in range(3):
+            deal(which, k).wait_send()
+
+
+def pool_kernel(
+    seqs, batch, g_ref, w_ref, r_ref, gain_ref, o_ref, res_ref, x_ref, cb, pb, cs, cr, ws, wr, bs, br, ys, yr, ps, pr, hs, hr, ls
+):
     s, d = lax.axis_index("seq"), lax.axis_index("dp")
     far, near = flip(s, 2), flip(s, 1)
     half = x_ref.shape[0] // 2
     low, high = pl.ds(0, half), pl.ds(half, half)
-    greet(neighbours(s, d, batch))
+    mates = [(True, {"seq": near, "dp": d}), (True, {"seq": far, "dp": d})]
+    for k in range(1, batch):
+        mates.append((True, {"seq": s, "dp": lax.rem(d + k, batch)}))
+    greet(mates)
+
+    def hand(k):
+        to = lax.rem(d + k, batch)
+        return remote(cb.at[to], pb.at[d], cs.at[k], cr.at[k], seq=s, dp=to)
+
+    tokens, width = x_ref.shape
+    part = width // batch
+    block = jnp.dot(
+        g_ref[...].reshape(batch * tokens, width), w_ref[...], preferred_element_type=jnp.float32
+    )
+    cb[...] = block.astype(jnp.bfloat16).reshape(batch, tokens, part)
+    for k in range(1, batch):
+        hand(k).start()
+    mine = pltpu.make_async_copy(cb.at[d], pb.at[d], ls.at[1])
+    mine.start()
+    for k in range(1, batch):
+        hand(k).wait_recv()
+    mine.wait()
+    squares = jnp.zeros((tokens, 1), jnp.float32)
+    for p in range(batch):
+        at = pl.ds(p * part, part)
+        stream = (r_ref[:, at].astype(jnp.float32) + pb[p].astype(jnp.float32)).astype(jnp.bfloat16)
+        res_ref[:, at] = stream
+        stream = stream.astype(jnp.float32)
+        squares += jnp.sum(stream * stream, axis=-1, keepdims=True)
+    scale = lax.rsqrt(squares / width + norm_eps)
+    x_ref[...] = (res_ref[...].astype(jnp.float32) * scale * gain_ref[...]).astype(jnp.bfloat16)
 
     def at(ss, dd):
         return o_ref.at[ss * batch + dd]
@@ -295,6 +398,8 @@
         beside_far(block, 0).wait_send()
         beside_far(block, 1).wait_send()
     own.wait()
+    for k in range(1, batch):
+        hand(k).wait_send()
 
 
 def scatter_kernel(
@@ -421,36 +526,52 @@
     )
 
 
-def line_gather(x, table):
+def attend_gather(queries_keys, values, documents, table):
     seqs, batch = lax.axis_size("seq"), lax.axis_size("dp")
     n = seqs * batch
+    tokens, width = values.shape
     return pl.pallas_call(
         functools.partial(line_kernel, seqs, batch),
         out_shape=(
-            jax.ShapeDtypeStruct((batch,) + x.shape, x.dtype),
+            jax.ShapeDtypeStruct((batch, tokens, width), values.dtype),
             jax.ShapeDtypeStruct((n,) + table.shape, table.dtype),
         ),
-        in_specs=[VMEM, VMEM],
+        in_specs=[VMEM] * 5,
         out_specs=(VMEM, VMEM),
         scratch_shapes=[
+            pltpu.VMEM((3, seqs * tokens, width // seqs), values.dtype),
+            pltpu.VMEM((seqs * tokens, width // seqs), values.dtype),
             DMA((2, batch)),
             DMA((2, batch)),
             DMA((n,)),
             DMA((n,)),
-            DMA((2,)),
+            DMA((5,)),
+            DMA((3, seqs)),
+            DMA((3, seqs)),
+            DMA((seqs,)),
+            DMA((seqs,)),
         ],
         compiler_params=params(1),
-    )(x, table)
-
-
-def pool_gather(x):
+    )(queries_keys, values, documents[None, :], documents[:, None], table)
+
+
+def pool_gather(gathered, weight, resid, gain):
     seqs, batch = lax.axis_size("seq"), lax.axis_size("dp")
+    tokens, width = resid.shape
     return pl.pallas_call(
         functools.partial(pool_kernel, seqs, batch),
-        out_shape=jax.ShapeDtypeStruct((seqs * batch,) + x.shape, x.dtype),
-        in_specs=[VMEM],
-        out_specs=VMEM,
+        out_shape=(
+            jax.ShapeDtypeStruct((seqs * batch,) + resid.shape, resid.dtype),
+            jax.ShapeDtypeStruct(resid.shape, resid.dtype),
+        ),
+        in_specs=[VMEM] * 4,
+        out_specs=(VMEM, VMEM),
         scratch_shapes=[
+            pltpu.VMEM(resid.shape, resid.dtype),
+            pltpu.VMEM((batch, tokens, width // batch), resid.dtype),
+            pltpu.VMEM((batch, tokens, width // batch), resid.dtype),
+            DMA((batch,)),
+            DMA((batch,)),
             DMA((2, batch)),
             DMA((2, batch)),
             DMA((2, batch)),
@@ -461,10 +582,10 @@
             DMA((batch,)),
             DMA((2, batch)),
             DMA((2, batch)),
-            DMA((1,)),
+            DMA((2,)),
         ],
         compiler_params=params(2),
-    )(x)
+    )(gathered, weight, resid, gain[None, :])
 
 
 def pool_scatter(x):
@@ -493,10 +614,10 @@
     )(x)
 
 
-def gathered_layer(residual, normed, table, gate, up, down, shared, score):
+def gathered_layer(residual, pool, table, gate, up, down, shared, score):
     seq_count, batch_count = lax.axis_size("seq"), lax.axis_size("dp")
     devices = seq_count * batch_count
-    tokens, width = normed.shape
+    tokens, width = residual.shape
     own_experts = gate.shape[0] // SPLIT
     room = devices * CAP
     me = lax.axis_index("seq") * batch_count + lax.axis_index("dp")
@@ -513,7 +634,7 @@
     slot_gate = jnp.sum(jnp.where(pick, weight.T[:, None, :], 0.0), axis=-1)
     pick = pick.astype(jnp.bfloat16).reshape(own_experts * room, total)
 
-    pool = pool_gather(normed).reshape(total, width)
+    pool = pool.reshape(total, width)
     rows = jnp.dot(pick, pool, preferred_element_type=jnp.float32).astype(jnp.bfloat16)
     rows = rows.reshape(own_experts, room, width)
     gate = gate.reshape((own_experts, SPLIT) + gate.shape[1:])
@@ -563,6 +684,23 @@
     tokens = resid.shape[1]
     model_width = resid.shape[2]
     local_heads = model_width // HD // seq_count
+    dense = expert_gate.shape[0] % SPLIT == 0 and seq_count == 4 and batch_count > 1
+    if dense and tokens % 32 == 0:
+        table = jnp.concatenate([expert_ids[0].astype(jnp.float32), gate_vals[0]], axis=1)
+        table = jnp.pad(table.T, ((0, 0), (0, -tokens % 128)))
+        gathered, table = attend_gather(queries_keys[:, 0], values[0], doc_ids[0], table)
+        table = table[:, :, :tokens].swapaxes(1, 2).reshape(-1, 2 * TOPK)
+        pool, residual = pool_gather(gathered, out_weight, resid[0], norm_gain)
+        return gathered_layer(
+            residual,
+            pool,
+            table,
+            expert_gate,
+            expert_up,
+            expert_down,
+            (shared_gate, shared_up, shared_down),
+            shared_score,
+        )
     paired = queries_keys.reshape(2, tokens, seq_count, local_heads, HD)
     valued = values.reshape(1, tokens, seq_count, local_heads, HD)
     documents = doc_ids[0]
@@ -575,15 +713,7 @@
     own_attended = lax.all_to_all(
         by_position, "seq", split_axis=0, concat_axis=2, tiled=True
     ).reshape(tokens, model_width)
-    dense = expert_gate.shape[0] % SPLIT == 0 and seq_count == 4 and batch_count > 1 and tokens % 32 == 0
-    if dense:
-        table = jnp.concatenate([expert_ids[0].astype(jnp.float32), gate_vals[0]], axis=1)
-        table = jnp.pad(table.T, ((0, 0), (0, -tokens % 128)))
-        gathered, table = line_gather(own_attended, table)
-        gathered = gathered.reshape(batch_count * tokens, model_width)
-        table = table[:, :, :tokens].swapaxes(1, 2).reshape(-1, 2 * TOPK)
-    else:
-        gathered = lax.all_gather(own_attended, "dp", axis=0, tiled=True)
+    gathered = lax.all_gather(own_attended, "dp", axis=0, tiled=True)
     column_block = jnp.dot(
         gathered,
         out_weight,
@@ -595,17 +725,6 @@
     normed = (
         stream * lax.rsqrt(jnp.mean(stream * stream, axis=-1, keepdims=True) + norm_eps) * norm_gain
     ).astype(jnp.bfloat16)
-    if dense:
-        return gathered_layer(
-            residual,
-            normed,
-            table,
-            expert_gate,
-            expert_up,
-            expert_down,
-            (shared_gate, shared_up, shared_down),
-            shared_score,
-        )
     shared_parts = shared_block(
         lax.all_gather(normed, "dp", axis=0, tiled=True), shared_gate, shared_up, shared_down
     )

time: 194 us -> 176 us (0.907)
  Pallas kernels: 99.5 us -> 125 us
  waiting for transfers between devices: 21.6 us -> 0 us
  starting transfers between devices: 14.9 us -> 0 us
  matrix products: 45.2 us -> 40.7 us
    pallas_call x2, Pallas kernels: 56.4 us -> 81.8 us  [the longest x1 44.2 us: attend_gather(): pl.pallas_call(functools.partial(line_kernel, seqs, batch), out_shape=(ja...]
    all_to_all x4 -> x0, waiting for transfers between devices: 21.6 us -> none  [the longest x1 6.8 us: body(): lax.all_to_all(paired, 'seq', split_axis=2, concat_axis=1, tiled=True)]
    all_to_all x4 -> x0, starting transfers between devices: 14.9 us -> none  [the longest x1 4.27 us: body(): lax.all_to_all(valued, 'seq', split_axis=2, concat_axis=1, tiled=True)]
    dot_general x3 -> x0, matrix products: 6.41 us -> none  [the longest x1 3 us: body(): jnp.dot(gathered, out_weight, preferred_element_type=jnp.float32)]
    unnamed x26 -> x21, local copies, waits for them, and re-layouts: 0.11 us -> 5.92 us
    reshape x5 -> x0, local copies, waits for them, and re-layouts: 5.17 us -> none  [the longest x2 2.33 us: body(): paired = queries_keys.reshape(2, tokens, seq_count, local_heads, HD)]
  transfers between devices with their start and end apart: 4 -> 0, of which waited for: 4 -> 0; matrix products, arithmetic and copies ran while one was open for 3% -> 0% of each run, Pallas kernels for 0% -> 0%
where the time goes in v3:
time: 176 us
  Pallas kernels  125 us (71%)
  matrix products  40.7 us (23%)
  local copies, waits for them, and re-layouts  7.09 us (4%)
  other arithmetic  2.98 us (2%)
    pallas_call x1, Pallas kernels, attend_gather(): pl.pallas_call(functools.partial(line_kernel, seqs, batch), out_shape=(ja...  44.2 us
    pallas_call x1, Pallas kernels, pool_scatter(): pl.pallas_call(functools.partial(scatter_kernel, seqs, batch), out_shape=...  43.2 us
    pallas_call x1, Pallas kernels, pool_gather(): pl.pallas_call(functools.partial(pool_kernel, seqs, batch), out_shape=(ja...  37.6 us
    dot_general x1, matrix products, gathered_layer(): jnp.einsum('ecd,ebdf->ebcf', rows, up, preferred_element_type=jnp.float32)  8.24 us
    dot_general x1, matrix products, gathered_layer(): jnp.einsum('ebcf,ebfd->ecd', hidden, down, preferred_element_type=jnp.flo...  7.64 us
    dot_general x1, matrix products, shared_block(): return jnp.dot(hidden, down_matrix, preferred_element_type=jnp.float32)  6.92 us
    dot_general x1, matrix products, gathered_layer(): jnp.einsum('ecd,ebdf->ebcf', rows, gate, preferred_element_type=jnp.float32)  6.86 us
    unnamed x21, local copies, waits for them, and re-layouts  5.92 us

profile of v3, /device:TPU:0, one launch (start us, length us, event | category | flops | bytes accessed | tf_op | source)
XLA Modules:
  0.0 176.0 jit_solution(3300486843480166788)
XLA Ops:
  0.0 0.0 copy-start
  0.0 1.0 copy.21.col_ref
  1.0 0.7 convert_bitcast_fusion
  1.7 0.7 maximum_bitcast_fusion
  2.4 0.0 copy-start.2
  2.4 1.0 copy-done.2
  3.4 0.0 copy-start.4
  3.4 0.9 copy-done.4
  4.3 0.0 copy-start.7
  4.3 0.7 copy-done.7
  5.0 44.2 %shard_map.145 = (bf16[4,64,2048]{2,1,0:T(8,128)(2,1)S(1)}, f32[16,8,128]{2,1,0:T(8,128)S(1)}) custom-call(bf16[2,64,2048]{2,1,0:T(8,128)(2,1)S(1)} %bitcast.79, bf16[64,2048]{1,0:T(8,128)(2,1)S(1)} %bitcast.84, s32[1,256]{1,0:T(1,128)S(1)} %copy-done.7, s32[256,1]{1,0:T(8,128)S(1)} %copy.21.col_ref, f32[8,128]{1,0:T(8,128)S(1)} %pad.4.t_ref), custom_call_target="tpu_custom_call" | custom-call | tf_op jit(solution)/shard_map/pallas_call | solution.py:533
  49.3 0.0 copy-start.1
  49.3 1.6 copy-done.1
  50.8 0.0 copy-start.5
  50.8 0.9 copy-done.5
  51.8 0.0 copy-start.6
  51.8 0.7 copy-done.6
  52.5 0.0 copy-start.9
  52.5 37.6 %shard_map.146 = (bf16[16,64,2048]{2,1,0:T(8,128)(2,1)S(1)}, bf16[64,2048]{1,0:T(8,128)(2,1)S(1)}) custom-call(bf16[4,64,2048]{2,1,0:T(8,128)(2,1)S(1)} %get-tuple-element.9.g_ref, bf16[2048,512]{1,0:T(8,128)(2,1)S(1)} %copy-done.1, bf16[64,2048]{1,0:T(8,128)(2,1)S(1)} %bitcast.85, f32[1,2048]{1,0:T(1,128)S(1)} %bitcast.86), custom_call_target="tpu_custom_call" | custom-call | tf_op jit(solution)/shard_map/pallas_call | solution.py:561
  90.1 0.0 copy-start.3
  90.1 0.0 copy-start.8
  90.1 0.0 copy-done.9
  90.1 2.1 %fusion.15 = f32[256,704]{0,1:T(8,128)} fusion(bf16[2048,704]{0,1:T(8,128)(2,1)S(1)} %copy-done.9, bf16[1024,2048]{1,0:T(8,128)(2,1)S(1)} %bitcast.80, s32[]{:T(128)S(6)} %select_n.18), kind=kOutput, calls=%fused_computation.27 | convolution fusion | flops 738197504 | bytes 4653060 | tf_op jit(solution)/shard_map/dot_general | solution.py:59
  92.3 0.0 copy-done.8
  92.3 0.4 fusion.12
  92.7 0.0 copy-done.3
  92.7 0.0 copy-done
  92.7 6.9 %convolution_multiply_fusion = f32[256,2048]{1,0:T(8,128)} fusion(bf16[704,2048]{1,0:T(8,128)(2,1)S(1)} %copy-done, f32[256]{0:T(256)S(1)} %add_divide_fusion, bf16[2048,704]{0,1:T(8,128)(2,1)} %param.27, bf16[1024,2048]{1,0:T(8,128)(2,1)} %bitcast.82, s32[]{:T(128)S(6)} %select_n.18, f32[256,704]{0,1:T(8,128)} %fusion.15), kind=kOutput, calls=%fused_computation.6 | convolution fusion | flops 1478000640 | bytes 9634820 | tf_op jit(solution)/shard_map/dot_general | solution.py:62
  99.7 0.1 reshape.76
  99.7 0.1 fusion.27
  99.9 0.5 fusion.11
  100.3 0.2 iota_compare_fusion.2
  100.5 3.7 %convolution_convert_fusion = bf16[320,2048]{1,0:T(8,128)(2,1)S(1)} fusion(pred[320,1024]{1,0:T(32,128)(4,1)S(1)} %bitcast.92, bf16[1024,2048]{1,0:T(8,128)(2,1)} %bitcast.83), kind=kOutput, calls=%fused_computation.8 | convolution fusion | flops 1342832640 | bytes 5832704 | tf_op jit(solution)/shard_map/dot_general | solution.py:638
  104.3 6.9 %fusion.35 = f32[2,160,4,352]{3,1,2,0:T(8,128)S(1)} fusion(bf16[2,160,2048,1]{2,1,3,0:T(8,128)(2,1)S(1)} %bitcast.89, bf16[2,4,2048,352]{2,3,1,0:T(8,128)(2,1)} %bitcast.88), kind=kOutput, calls=%fused_computation.53 | convolution fusion | flops 1845493760 | bytes 14647296 | tf_op jit(solution)/shard_map/ecd,ebdf->ebcf/dot_general | solution.py:643
  111.1 8.2 %fusion.4 = bf16[2,4,160,352]{3,2,1,0:T(8,128)(2,1)S(1)} fusion(f32[2,160,4,352]{3,1,2,0:T(8,128)S(1)} %fusion.35, bf16[2,160,2048,1]{2,1,3,0:T(8,128)(2,1)S(1)} %bitcast.90, bf16[2,4,2048,352]{2,3,1,0:T(8,128)(2,1)} %bitcast.96), kind=kOutput, calls=%fused_computation.10 | convolution fusion | flops 1848197120 | bytes 15548416 | tf_op jit(solution)/shard_map/ecd,ebdf->ebcf/dot_general | solution.py:644
  119.4 0.2 select_reduce_fusion
  119.6 7.6 %fusion.3 = bf16[2,160,2048]{2,1,0:T(8,128)(2,1)} fusion(bf16[2,4,160,352]{3,2,1,0:T(8,128)(2,1)S(1)} %fusion.4, bf16[2,4,352,2048]{3,2,1,0:T(8,128)(2,1)} %bitcast.97, f32[2,160]{1,0:T(2,128)S(1)} %select_reduce_fusion), kind=kOutput, calls=%fused_computation.7 | convolution fusion | flops 1846804480 | bytes 13747456 | tf_op jit(solution)/shard_map/ebcf,ebfd->ecd/dot_general | solution.py:646
  127.2 0.1 eq.64
  127.3 0.3 bitcast_compare_fusion
  127.6 4.4 %fusion = bf16[4,256,2048]{2,1,0:T(8,128)(2,1)S(1)} fusion(f32[256,2048]{1,0:T(8,128)} %convolution_multiply_fusion, pred[4]{0:T(512)(128)(4,1)S(1)} %iota_compare_fusion.5, bf16[320,2048,1]{1,0,2:T(8,128)(2,1)} %bitcast.98, pred[40,4,8,256]{3,2,1,0:T(8,128)(4,1)S(1)} %bitcast.91), kind=kOutput, calls=%fused_computation.1 | convolution fusion | flops 1348468736 | bytes 7929860 | tf_op jit(solution)/shard_map/dot_general | solution.py:648
  132.0 43.2 %shard_map.147 = bf16[64,2048]{1,0:T(8,128)(2,1)S(1)} custom-call(bf16[16,64,2048]{2,1,0:T(8,128)(2,1)S(1)} %bitcast.78), custom_call_target="tpu_custom_call" | custom-call | tf_op jit(solution)/shard_map/pallas_call | solution.py:595
  175.2 0.8 fusion.25
  (9 shorter events, 0.1 us)
Async XLA Ops:
  0.0 92.7 %copy-start = (bf16[704,2048]{1,0:T(8,128)(2,1)S(1)}, bf16[704,2048]{1,0:T(8,128)(2,1)}, u32[]{:S(2)}) copy-start(bf16[704,2048]{1,0:T(8,128)(2,1)} %param.28) | copy-start | bytes 8650756
  2.4 1.0 copy-start.2
  3.4 0.9 copy-start.4
  4.3 0.7 copy-start.7
  49.3 1.6 copy-start.1
  50.8 0.9 copy-start.5
  51.8 0.7 copy-start.6
  52.5 37.6 %copy-start.9 = (bf16[2048,704]{0,1:T(8,128)(2,1)S(1)}, bf16[2048,704]{0,1:T(8,128)(2,1)}, u32[]{:S(2)}) copy-start(bf16[2048,704]{0,1:T(8,128)(2,1)} %param.26) | copy-start | bytes 8650756
  90.1 2.6 %copy-start.3 = (bf16[16,64,2048]{2,1,0:T(8,128)(2,1)}, bf16[16,64,2048]{2,1,0:T(8,128)(2,1)S(1)}, u32[]{:S(2)}) copy-start(bf16[16,64,2048]{2,1,0:T(8,128)(2,1)S(1)} %get-tuple-element.12) | copy-start | bytes 12582916
  90.1 2.2 %copy-start.8 = (bf16[2048]{0:T(1024)(128)(2,1)S(1)}, bf16[2048]{0:T(1024)(128)(2,1)}, u32[]{:S(2)}) copy-start(bf16[2048]{0:T(1024)(128)(2,1)} %param.29) | copy-start | bytes 12292
